TPU v7x, 512 devices: a whole 4x8x8 slice. The times are simulated.
512 devices in a mesh: resp: 64 (over y, z), head: 8 (over x, core).
Axes of the slice: x: 4, y: 8, z: 8, core: 2. Of those that a mesh axis runs over, the one named last changes fastest.
Arguments:
- queries: bfloat16 [8192, 24576], P('resp', 'head'), may hold values from -8 to 8
- resp_latent: bfloat16 [8192, 576], P('resp'), may hold values from -8 to 8
- prompt_latent: bfloat16 [64, 128, 576], P('resp'), may hold values from -6 to 6
- up_keys: bfloat16 [128, 128, 512], P('head', None, 'resp'), may hold values from -0.5 to 0.5
- up_values: bfloat16 [128, 512, 128], P('head', 'resp'), may hold values from -0.25 to 0.25
- cotangent: bfloat16 [8192, 16384], P('resp', 'head'), may hold values from -6 to 6
- prompt_len: int32 [32], replicated, may hold values from 32 to 128
- resp_len: int32 [128], replicated, may hold values from 16 to 64
- resp_count: int32 [32], replicated, may hold values from 1 to 8, 128 in all
- owner: int32 [32], replicated, may hold values from 0 to 63, as said below
Outputs:
- attended: bfloat16 [8192, 16384], P('resp', 'head')
- grad_queries: bfloat16 [8192, 24576], P('resp', 'head')
- grad_response: float32 [8192, 576], P('resp', 'head')
- grad_prompt: float32 [64, 128, 576], P('resp', None, 'head')
Inputs may be any that keep to these rules, and one draw needn't show every extreme that they name: Distinct slots; prompt p's cache is prompt_latent[owner[p]]. `resp_count`: every prompt has at least one response; they sum to 128.
All inputs are finite; a program needn't handle non-finite values.
Results may differ from a plain program's by a relative error of at most 0.014.
Values may be sent and summed in bfloat16 or wider, within the bound.
No kernel may reach another device: no remote copies, remote signals or barrier semaphores. Data moves between devices by JAX's collectives and lax.ppermute only.
A program may use at most 64 MiB of HBM per device.

v0:
```python
import math

import jax
import jax.numpy as jnp
from jax import lax
from jax.sharding import PartitionSpec as P


def turned_gather(arrays, axis, dims):
    turned = [jnp.moveaxis(a, dim, 0) for a, dim in zip(arrays, dims)]
    both = jnp.concatenate([t.reshape(len(t), -1) for t in turned], axis=1)
    out, at, done = (lax.all_gather(both, axis, axis=0, tiled=True), 0, [])
    for t, dim in zip(turned, dims):
        piece = out[:, at : at + t[0].size].reshape(-1, *t.shape[1:])
        done.append(jnp.moveaxis(piece, 0, dim))
        at += t[0].size
    return tuple(done)


def in_order(tiles, dim):
    tiles = jnp.moveaxis(tiles, 0, dim)
    lengths = tiles.shape
    return tiles.reshape(*lengths[:dim], lengths[dim] * lengths[dim + 1], *lengths[dim + 2 :])


def sent_to_all(array, axis):
    copies = jnp.broadcast_to(array, (lax.axis_size(axis), *array.shape))
    return lax.all_to_all(copies, axis, split_axis=0, concat_axis=0, tiled=True)


def gathered_copies(array, axis, dim):
    return in_order(sent_to_all(array, axis), dim)


def split_up(array, dim, length):
    before, after = (array.shape[:dim], array.shape[dim + 1 :])
    return jnp.moveaxis(array.reshape(*before, length, -1, *after), dim, 0)


def sent_and_summed(array, axis, dim):
    length = lax.axis_size(axis)
    tiles = lax.all_to_all(split_up(array, dim, length), axis, 0, 0, tiled=True)
    return jnp.sum(tiles.astype(jnp.float32), axis=0)


def product(form, left, right):
    return jnp.einsum(form, left, right, preferred_element_type=jnp.float32)


def attend(queries, key_rows, key_valid, row_live, cotangent, up_keys, up_values):
    head_count, nope_width, latent_width = up_keys.shape
    row_count = queries.shape[0]
    split_query = queries.reshape(row_count, head_count, -1)
    score_scale = 1.0 / math.sqrt(split_query.shape[2])
    query_latent = product("thn,hnc->thc", split_query[:, :, :nope_width], up_keys).astype(
        jnp.bfloat16
    )
    query_full = jnp.concatenate([query_latent, split_query[:, :, nope_width:]], axis=2)
    scores = product("thc,kc->thk", query_full, key_rows) * score_scale
    scores = jnp.where(key_valid[:, None, :], scores, -jnp.inf)
    row_max = jnp.max(scores, axis=2, keepdims=True)
    expo = jnp.exp(scores - row_max)
    weights = expo / jnp.sum(expo, axis=2, keepdims=True)
    weights_bf = weights.astype(jnp.bfloat16)
    value_rows = key_rows[:, :latent_width]
    latent_out = product("thk,kc->thc", weights_bf, value_rows).astype(jnp.bfloat16)
    attended = product("thc,hcv->thv", latent_out, up_values) * row_live[:, None, None]
    grad_out = cotangent.reshape(row_count, head_count, -1)
    grad_latent = (product("thv,hcv->thc", grad_out, up_values) * row_live[:, None, None]).astype(
        jnp.bfloat16
    )
    grad_weights = product("thc,kc->thk", grad_latent, value_rows)
    inner = jnp.sum(weights * grad_weights, axis=2, keepdims=True)
    grad_scores = (weights * (grad_weights - inner) * score_scale).astype(jnp.bfloat16)
    grad_full = product("thk,kc->thc", grad_scores, key_rows)
    grad_nope = product(
        "thc,hnc->thn", grad_full[:, :, :latent_width].astype(jnp.bfloat16), up_keys
    )
    grad_query = jnp.concatenate([grad_nope, grad_full[:, :, latent_width:]], axis=2)
    grad_key = product("thk,thc->kc", grad_scores, query_full)
    grad_value = product("thk,thc->kc", weights_bf, grad_latent)
    grad_key = grad_key + jnp.pad(grad_value, ((0, 0), (0, key_rows.shape[1] - latent_width)))
    return (
        attended.reshape(row_count, -1).astype(jnp.bfloat16),
        grad_query.reshape(row_count, -1).astype(jnp.bfloat16),
        grad_key,
    )


def body(
    queries,
    resp_latent,
    prompt_latent,
    up_keys,
    up_values,
    cotangent,
    prompt_len,
    resp_len,
    resp_count,
    owner,
):
    resp_devices = lax.axis_size("resp")
    head_devices = lax.axis_size("head")
    my_index = lax.axis_index("resp")
    head_index = lax.axis_index("head")
    keys_full, values_full = turned_gather((up_keys, up_values), "resp", (2, 1))
    resp_total = resp_len.shape[0]
    per_device = resp_total // resp_devices
    row_count = queries.shape[0] // per_device
    prompt_rows = prompt_latent.shape[1]
    piece_rows = prompt_rows // resp_devices
    latent_cols = prompt_latent.shape[2]
    starts = jnp.cumsum(resp_count) - resp_count
    numbers = jnp.arange(resp_total, dtype=jnp.int32)
    prompt_of = jnp.sum((starts[None, :] <= numbers[:, None]).astype(jnp.int32), axis=1) - 1
    chosen = prompt_of[:, None] == jnp.arange(prompt_len.shape[0], dtype=jnp.int32)[None, :]
    slot_of = jnp.sum(jnp.where(chosen, owner[None, :], 0), axis=1)
    plen_of = jnp.sum(jnp.where(chosen, prompt_len[None, :], 0), axis=1)
    plen_mine = lax.dynamic_slice_in_dim(plen_of, my_index * per_device, per_device)
    rlen_mine = lax.dynamic_slice_in_dim(resp_len, my_index * per_device, per_device)
    col_share = latent_cols // head_devices
    latent_share = lax.dynamic_slice_in_dim(prompt_latent, head_index * col_share, col_share, 2)
    stripes = lax.all_to_all(latent_share, "resp", split_axis=1, concat_axis=0, tiled=True)
    outgoing = jnp.take(stripes, slot_of, axis=0)
    outgoing = outgoing.reshape(resp_devices, per_device, piece_rows, stripes.shape[2])
    fetched = lax.all_to_all(outgoing, "resp", split_axis=0, concat_axis=2, tiled=True)[0]
    fetched = gathered_copies(fetched, "head", 2)
    own_rows = resp_latent.reshape(per_device, row_count, latent_cols)
    key_rows = jnp.concatenate([fetched, own_rows], axis=1)
    positions = jnp.arange(row_count, dtype=jnp.int32)
    prompt_pos = jnp.arange(prompt_rows, dtype=jnp.int32)
    prompt_ok = jnp.broadcast_to(
        prompt_pos[None, None, :] < plen_mine[:, None, None], (per_device, row_count, prompt_rows)
    )
    causal = jnp.broadcast_to(
        positions[None, :, None] >= positions[None, None, :], (per_device, row_count, row_count)
    )
    key_valid = jnp.concatenate([prompt_ok, causal], axis=2)
    row_live = (positions[None, :] < rlen_mine[:, None]).astype(jnp.float32)
    query_blocks = queries.reshape(per_device, row_count, -1)
    grad_blocks = cotangent.reshape(per_device, row_count, -1)
    attended, grad_query, grad_key = jax.vmap(attend, in_axes=(0, 0, 0, 0, 0, None, None))(
        query_blocks, key_rows, key_valid, row_live, grad_blocks, keys_full, values_full
    )
    grad_prompt_rows = grad_key[:, :prompt_rows]
    grad_own = grad_key[:, prompt_rows:].reshape(per_device * row_count, latent_cols)
    grad_prompt_rows, grad_own = (
        sent_and_summed(grad_prompt_rows.astype(jnp.bfloat16), "head", 2),
        sent_and_summed(grad_own.astype(jnp.bfloat16), "head", 1),
    )
    sent_cols = grad_prompt_rows.shape[2]
    arrived = lax.all_to_all(
        grad_prompt_rows[None].astype(jnp.bfloat16), "resp", split_axis=2, concat_axis=0, tiled=True
    ).astype(jnp.float32)
    flat_rows = arrived.reshape(resp_devices * per_device, piece_rows * sent_cols)
    slot_table = (slot_of[None, :] == jnp.arange(resp_devices, dtype=jnp.int32)[:, None]).astype(
        jnp.float32
    )
    summed = jnp.dot(slot_table, flat_rows, precision=lax.Precision.HIGHEST)
    summed = summed.reshape(resp_devices, piece_rows, sent_cols)
    at_owner = lax.all_to_all(
        summed.astype(jnp.bfloat16), "resp", split_axis=0, concat_axis=1, tiled=True
    ).astype(summed.dtype)
    return (
        attended.reshape(per_device * row_count, -1),
        grad_query.reshape(per_device * row_count, -1),
        grad_own,
        at_owner,
    )


def solution(mesh):
    placed = (
        P("resp", "head"),
        P("resp", None),
        P("resp", None, None),
        P("head", None, "resp"),
        P("head", "resp", None),
        P("resp", "head"),
        P(),
        P(),
        P(),
        P(),
    )
    return jax.shard_map(
        body,
        mesh=mesh,
        in_specs=placed,
        out_specs=(
            P("resp", "head"),
            P("resp", "head"),
            P("resp", "head"),
            P("resp", None, "head"),
        ),
        check_vma=False,
    )
```

profile of v0, /device:TPU:1, one launch (start us, length us, event | category | flops | bytes accessed | tf_op | source)
XLA Modules:
  0.0 217.1 jit_solution(1038570056481774946)
XLA Ops:
  7.2 1.5 pad_maximum_fusion.3
  8.8 0.8 copy.159
  9.5 17.1 %all-to-all-start = ((bf16[1,128,72]{2,0,1:T(2,128)(2,1)}), bf16[1,128,72]{2,0,1:T(2,128)(2,1)S(1)}, u32[]{:S(2)}, u32[]{:S(2)}) async-start(bf16[1,128,72]{2,0,1:T(2,128)(2,1)} %copy.159), calls=%async_computation | async-start | bytes 131072 | tf_op jit(solution)/shard_map/all_to_all | solution.py:123
  26.7 0.7 copy.118
  28.3 0.8 select_reduce_fusion.1
  29.4 8.4 %all-to-all-done = bf16[1,128,72]{2,0,1:T(2,128)(2,1)S(1)} async-done(((bf16[1,128,72]{2,0,1:T(2,128)(2,1)}), bf16[1,128,72]{2,0,1:T(2,128)(2,1)S(1)}, u32[]{:S(2)}, u32[]{:S(2)}) %all-to-all-start) | async-done | bytes 18464 | tf_op jit(solution)/shard_map/all_to_all | solution.py:123
  37.8 0.7 gather_fusion
  38.5 0.8 broadcast_select_fusion
  39.4 4.6 %all-to-all-start.1 = ((bf16[64,2,2,72]{3,2,1,0:T(2,128)(2,1)}), bf16[64,2,2,72]{3,2,1,0:T(2,128)(2,1)S(1)}, u32[]{:S(2)}, u32[]{:S(2)}) async-start(bf16[64,2,2,72]{3,2,1,0:T(2,128)(2,1)} %broadcast_select_fusion), calls=%async_computation.1 | async-start | bytes 131072 | tf_op jit(solution)/shard_map/all_to_all | solution.py:126
  44.0 11.2 %all-to-all-done.1 = bf16[64,2,2,72]{3,2,1,0:T(2,128)(2,1)S(1)} async-done(((bf16[64,2,2,72]{3,2,1,0:T(2,128)(2,1)}), bf16[64,2,2,72]{3,2,1,0:T(2,128)(2,1)S(1)}, u32[]{:S(2)}, u32[]{:S(2)}) %all-to-all-start.1) | async-done | bytes 36896 | tf_op jit(solution)/shard_map/all_to_all | solution.py:126
  55.4 0.8 broadcast_in_dim.82
  56.1 7.5 %all-to-all-start.2 = ((bf16[8,2,128,72]{2,3,1,0:T(8,128)(2,1)}), bf16[8,2,128,72]{2,3,1,0:T(8,128)(2,1)}, u32[]{:S(2)}, u32[]{:S(2)}) async-start(bf16[8,2,128,72]{2,3,1,0:T(8,128)(2,1)} %broadcast_in_dim.82), calls=%async_computation.2 | async-start | bytes 589824 | tf_op jit(solution)/shard_map/all_to_all | solution.py:28
  63.7 1.1 reshape_reshape.6
  65.7 0.9 copy.160
  66.7 3.8 %all-to-all-done.2 = bf16[8,2,128,72]{2,3,1,0:T(8,128)(2,1)} async-done(((bf16[8,2,128,72]{2,3,1,0:T(8,128)(2,1)}), bf16[8,2,128,72]{2,3,1,0:T(8,128)(2,1)}, u32[]{:S(2)}, u32[]{:S(2)}) %all-to-all-start.2) | async-done | bytes 294944 | tf_op jit(solution)/shard_map/all_to_all | solution.py:28
  70.5 1.0 copy.125
  71.5 0.9 copy.127
  72.4 26.7 %all-gather.2.cloned.1.call-done = bf16[512,4096]{1,0:T(8,128)(2,1)} async-done(((bf16[8,4096]{1,0:T(8,128)(2,1)}), bf16[512,4096]{1,0:T(8,128)(2,1)}) %all-gather.2.cloned.1.call-update) | async-done | bytes 4194320 | tf_op jit(solution)/shard_map/all_gather | solution.py:12
  99.2 4.8 %fusion.55 = (bf16[512,2048]{1,0:T(8,128)(2,1)}, bf16[512,2048]{1,0:T(8,128)(2,1)}) fusion(bf16[512,4096]{1,0:T(8,128)(2,1)} %all-gather.2.cloned.1.call-done), kind=kLoop, calls=%fused_computation.79 | loop fusion | bytes 8388608 | tf_op jit(solution)/shard_map/slice | solution.py:14
  104.0 2.9 %copy.116 = bf16[512,2048]{0,1:T(8,128)(2,1)S(1)} copy(bf16[512,2048]{1,0:T(8,128)(2,1)} %get-tuple-element.22) | data formatting | bytes 4194304 | tf_op jit(solution)/shard_map/slice | solution.py:14
  106.8 2.4 %copy.117 = bf16[512,16,128]{2,0,1:T(8,128)(2,1)} copy(bf16[512,16,128]{0,2,1:T(8,128)(2,1)S(1)} %bitcast.123) | data formatting | bytes 4194304 | tf_op jit(solution)/shard_map/reshape | solution.py:14
  109.3 2.9 %copy.119 = bf16[512,2048]{0,1:T(8,128)(2,1)S(1)} copy(bf16[512,2048]{1,0:T(8,128)(2,1)} %get-tuple-element.23) | data formatting | bytes 4194304 | tf_op jit(solution)/shard_map/slice | solution.py:14
  112.1 1.7 fusion.66
  114.2 1.9 pad_maximum_fusion
  116.1 5.2 %fusion.56 = (f32[2,64,16]{2,1,0:T(8,128)S(1)}, f32[2,64,16,192]{3,2,1,0:T(8,128)}) fusion(pred[2,64,192]{2,1,0:T(8,128)(4,1)S(1)} %pad_add_fusion, bf16[2,64,16,576]{3,1,0,2:T(8,128)(2,1)} %pad_maximum_fusion, bf16[2,64,576]{2,1,0:T(8,128)(2,1)S(1)} %bitcast.134, bf16[2,128,576]{2,1,0:T(8,128)(2,1)} %copy.127), kind=kOutput, calls=%fused_computation.80 | convolution fusion | flops 455442624 | bytes 4407296 | tf_op jit(solution)/shard_map/vmap()/sub | solution.py:62
  121.3 2.0 fusion.54
  123.3 0.7 convolution_convert_fusion.1
  124.0 0.9 copy-done.1
  126.3 0.7 fusion.22
  127.0 1.3 fusion.13
  128.6 11.3 %multiply_convert_fusion.1 = bf16[2,64,16,192]{3,2,1,0:T(8,128)(2,1)S(1)} fusion(f32[2,64,16,192]{3,2,1,0:T(8,128)S(1)} %fusion.13, f32[2,64,16,192]{3,2,1,0:T(8,128)S(1)} %copy-done.4, f32[2,64,16]{2,1,0:T(8,128)S(1)} %get-tuple-element.24), kind=kOutput, calls=%fused_computation.18 | output fusion | flops 2754751 | bytes 3940352 | tf_op jit(solution)/shard_map/vmap()/sub | solution.py:74
  139.9 0.9 fusion.28
  140.8 1.0 convolution_convert_fusion
  141.8 1.8 slice.48
  145.3 0.9 copy.191
  146.4 0.8 copy.143
  147.2 9.1 %all-to-all-start.4 = ((bf16[8,2,128,72]{2,3,1,0:T(8,128)(2,1)}), bf16[8,2,128,72]{2,3,1,0:T(8,128)(2,1)S(1)}, u32[]{:S(2)}, u32[]{:S(2)}) async-start(bf16[8,2,128,72]{2,3,1,0:T(8,128)(2,1)} %copy.143), calls=%async_computation.4 | async-start | bytes 589824 | tf_op jit(solution)/shard_map/all_to_all | solution.py:42
  156.6 0.8 copy.140
  157.4 2.8 %copy.133 = bf16[2,64,16,512]{3,1,0,2:T(8,128)(2,1)S(1)} copy(bf16[2,64,16,512]{3,2,1,0:T(8,128)(2,1)} %slice.48) | data formatting | bytes 4194304 | tf_op jit(solution)/shard_map/vmap()/slice | solution.py:77
  161.4 1.6 all-to-all-done.4
  163.1 0.7 copy.145
  163.8 8.0 %all-to-all-start.5 = ((bf16[1,2,128,72]{3,1,0,2:T(2,128)(2,1)}), bf16[1,2,128,72]{3,1,0,2:T(2,128)(2,1)S(1)}, u32[]{:S(2)}, u32[]{:S(2)}) async-start(bf16[1,2,128,72]{3,1,0,2:T(2,128)(2,1)} %copy.145), calls=%async_computation.5 | async-start | bytes 131072 | tf_op jit(solution)/shard_map/all_to_all | solution.py:152
  172.7 2.0 convert_element_type.102
  174.7 8.3 %all-to-all-done.5 = bf16[1,2,128,72]{3,1,0,2:T(2,128)(2,1)S(1)} async-done(((bf16[1,2,128,72]{3,1,0,2:T(2,128)(2,1)}), bf16[1,2,128,72]{3,1,0,2:T(2,128)(2,1)S(1)}, u32[]{:S(2)}, u32[]{:S(2)}) %all-to-all-start.5) | async-done | bytes 36896 | tf_op jit(solution)/shard_map/all_to_all | solution.py:152
  183.0 5.8 %all-to-all-start.3 = ((bf16[8,128,72]{1,2,0:T(8,128)(2,1)}), bf16[8,128,72]{1,2,0:T(8,128)(2,1)S(1)}, u32[]{:S(2)}, u32[]{:S(2)}) async-start(bf16[8,128,72]{1,2,0:T(8,128)(2,1)} %copy.140), calls=%async_computation.3 | async-start | bytes 294912 | tf_op jit(solution)/shard_map/all_to_all | solution.py:42
  189.9 4.3 %all-to-all-done.3 = bf16[8,128,72]{1,2,0:T(8,128)(2,1)S(1)} async-done(((bf16[8,128,72]{1,2,0:T(8,128)(2,1)}), bf16[8,128,72]{1,2,0:T(8,128)(2,1)S(1)}, u32[]{:S(2)}, u32[]{:S(2)}) %all-to-all-start.3) | async-done | bytes 147488 | tf_op jit(solution)/shard_map/all_to_all | solution.py:42
  194.2 4.6 %all-to-all-start.6 = ((bf16[64,2,72]{2,1,0:T(2,128)(2,1)}), bf16[64,2,72]{2,1,0:T(2,128)(2,1)S(1)}, u32[]{:S(2)}, u32[]{:S(2)}) async-start(bf16[64,2,72]{2,1,0:T(2,128)(2,1)} %copy.149), calls=%async_computation.6 | async-start | bytes 65536 | tf_op jit(solution)/shard_map/all_to_all | solution.py:161
  199.5 10.1 %all-to-all-done.6 = bf16[64,2,72]{2,1,0:T(2,128)(2,1)S(1)} async-done(((bf16[64,2,72]{2,1,0:T(2,128)(2,1)}), bf16[64,2,72]{2,1,0:T(2,128)(2,1)S(1)}, u32[]{:S(2)}, u32[]{:S(2)}) %all-to-all-start.6) | async-done | bytes 18464 | tf_op jit(solution)/shard_map/all_to_all | solution.py:161
  (79 shorter events, 11.1 us)
Async XLA Ops:
  7.2 1.6 copy-start
  7.2 56.5 %copy-start.7 = (bf16[128,3072]{1,0:T(8,128)(2,1)S(1)}, bf16[128,3072]{1,0:T(8,128)(2,1)}, u32[]{:S(2)}) copy-start(bf16[128,3072]{1,0:T(8,128)(2,1)} %param.10) | copy-start | bytes 2359300
  7.2 92.0 %all-gather.2.cloned.1.call-start = ((), (), s32[]{:S(2)}) async-start(), calls=%async_computation.7 | async-start | bytes 4259840 | tf_op jit(solution)/shard_map/all_gather | solution.py:12
  9.5 28.3 %all-to-all-start = ((bf16[1,128,72]{2,0,1:T(2,128)(2,1)}), bf16[1,128,72]{2,0,1:T(2,128)(2,1)S(1)}, u32[]{:S(2)}, u32[]{:S(2)}) async-start(bf16[1,128,72]{2,0,1:T(2,128)(2,1)} %copy.159), calls=%async_computation | async-start | bytes 131072 | tf_op jit(solution)/shard_map/all_to_all | solution.py:123
  39.4 15.9 %all-to-all-start.1 = ((bf16[64,2,2,72]{3,2,1,0:T(2,128)(2,1)}), bf16[64,2,2,72]{3,2,1,0:T(2,128)(2,1)S(1)}, u32[]{:S(2)}, u32[]{:S(2)}) async-start(bf16[64,2,2,72]{3,2,1,0:T(2,128)(2,1)} %broadcast_select_fusion), calls=%async_computation.1 | async-start | bytes 131072 | tf_op jit(solution)/shard_map/all_to_all | solution.py:126
  56.1 14.4 %all-to-all-start.2 = ((bf16[8,2,128,72]{2,3,1,0:T(8,128)(2,1)}), bf16[8,2,128,72]{2,3,1,0:T(8,128)(2,1)}, u32[]{:S(2)}, u32[]{:S(2)}) async-start(bf16[8,2,128,72]{2,3,1,0:T(8,128)(2,1)} %broadcast_in_dim.82), calls=%async_computation.2 | async-start | bytes 589824 | tf_op jit(solution)/shard_map/all_to_all | solution.py:28
  63.6 1.4 copy-start.10
  63.6 1.5 copy-start.9
  63.7 1.6 copy-start.8
  121.3 2.0 copy-start.5
  123.3 1.6 copy-start.1
  127.0 1.6 copy-start.4
  128.6 11.3 %copy-start.3 = (bf16[2,64,16,576]{3,1,0,2:T(8,128)(2,1)S(1)}, bf16[2,64,16,576]{3,1,0,2:T(8,128)(2,1)}, u32[]{:S(2)}) copy-start(bf16[2,64,16,576]{3,1,0,2:T(8,128)(2,1)} %pad_maximum_fusion) | copy-start | bytes 7077892
  140.8 1.0 copy-start.6
  141.8 2.2 copy-start.2
  144.7 1.5 slice-start.2
  144.9 11.4 %slice-start.1 = ((bf16[2,192,576]{2,1,0:T(8,128)(2,1)}), bf16[2,64,576]{2,1,0:T(8,128)(2,1)S(1)}, s32[]{:S(2)}) async-start(bf16[2,192,576]{2,1,0:T(8,128)(2,1)} %copy-done.6), calls=%async_computation.9 | async-start | bytes 327680 | tf_op jit(solution)/shard_map/slice | solution.py:146
  147.2 15.9 %all-to-all-start.4 = ((bf16[8,2,128,72]{2,3,1,0:T(8,128)(2,1)}), bf16[8,2,128,72]{2,3,1,0:T(8,128)(2,1)S(1)}, u32[]{:S(2)}, u32[]{:S(2)}) async-start(bf16[8,2,128,72]{2,3,1,0:T(8,128)(2,1)} %copy.143), calls=%async_computation.4 | async-start | bytes 589824 | tf_op jit(solution)/shard_map/all_to_all | solution.py:42
  160.1 1.0 slice-start
  163.8 19.2 %all-to-all-start.5 = ((bf16[1,2,128,72]{3,1,0,2:T(2,128)(2,1)}), bf16[1,2,128,72]{3,1,0,2:T(2,128)(2,1)S(1)}, u32[]{:S(2)}, u32[]{:S(2)}) async-start(bf16[1,2,128,72]{3,1,0,2:T(2,128)(2,1)} %copy.145), calls=%async_computation.5 | async-start | bytes 131072 | tf_op jit(solution)/shard_map/all_to_all | solution.py:152
  183.0 11.2 %all-to-all-start.3 = ((bf16[8,128,72]{1,2,0:T(8,128)(2,1)}), bf16[8,128,72]{1,2,0:T(8,128)(2,1)S(1)}, u32[]{:S(2)}, u32[]{:S(2)}) async-start(bf16[8,128,72]{1,2,0:T(8,128)(2,1)} %copy.140), calls=%async_computation.3 | async-start | bytes 294912 | tf_op jit(solution)/shard_map/all_to_all | solution.py:42
  194.2 15.4 %all-to-all-start.6 = ((bf16[64,2,72]{2,1,0:T(2,128)(2,1)}), bf16[64,2,72]{2,1,0:T(2,128)(2,1)S(1)}, u32[]{:S(2)}, u32[]{:S(2)}) async-start(bf16[64,2,72]{2,1,0:T(2,128)(2,1)} %copy.149), calls=%async_computation.6 | async-start | bytes 65536 | tf_op jit(solution)/shard_map/all_to_all | solution.py:161
Sparse Core Ops, SparseCore 0:
  11.0 88.1 all-gather.1
where the time goes:
time: 218 us; the launch traced here: 217 us
  waiting for transfers between devices  74.4 us (34%)
  starting transfers between devices  56.8 us (26%)
  local copies, waits for them, and re-layouts  36.1 us (17%)
  other arithmetic  21.5 us (10%)
  between operations  14.5 us (7%)
  matrix products  13.8 us (6%)
    all_gather x1, waiting for transfers between devices, turned_gather(): out, at, done = (lax.all_gather(both, axis, axis=0, tiled=True), 0, [])  26.7 us
    all_to_all x1, starting transfers between devices, body(): lax.all_to_all(latent_share, 'resp', split_axis=1, concat_axis=0, tiled=T...  17.1 us
    all_to_all x2, starting transfers between devices, sent_and_summed(): tiles = lax.all_to_all(split_up(array, dim, length), axis, 0, 0, tiled=True)  14.9 us
    sub x1, other arithmetic, attend(): grad_weights - inner  11.3 us
    all_to_all x1, waiting for transfers between devices, body(): lax.all_to_all(outgoing, 'resp', split_axis=0, concat_axis=2, tiled=True)[0]  11.2 us
    slice x3, local copies, waits for them, and re-layouts, turned_gather(): piece = out[:, at:at + t[0].size].reshape(-1, *t.shape[1:])  10.5 us
    all_to_all x1, waiting for transfers between devices, body(): lax.all_to_all(summed.astype(jnp.bfloat16), 'resp', split_axis=0, concat_...  10.1 us
    all_to_all x1, waiting for transfers between devices, body(): lax.all_to_all(latent_share, 'resp', split_axis=1, concat_axis=0, tiled=T...  8.36 us
  transfers between devices with their start and end apart: 8, of which 8 were waited for; matrix products, arithmetic and copies ran while one was open for 9% of the time, Pallas kernels for 0%

commit v1 on v0

v1 whole, which is shorter than its diff:
```python
import functools
import math

import jax
import jax.numpy as jnp
from jax import lax
from jax.experimental import pallas as pl
from jax.experimental.pallas import tpu as pltpu
from jax.sharding import PartitionSpec as P

F32, BF16 = jnp.float32, jnp.bfloat16
STEP_HEADS = 4


def dot(left, right, dims=((1,), (0,))):
    return lax.dot_general(left, right, (dims, ((), ())), preferred_element_type=F32)


NT, TN = ((1,), (1,)), ((0,), (0,))


def attend_kernel(
    sizes, plen, rlen, q_ref, ct_ref, wv_ref, wk_ref, kp_ref, ko_ref,
    out_ref, gq_ref, gk_ref, k_s, kt_s, qf_s, gl_s, lo_s, gf_s, acc_s,
):
    parts, rows, heads, nope, rope, val, lat, prows = sizes
    full, width, wide = lat + rope, nope + rope, k_s.shape[2]
    tokens = parts * rows
    step = pl.program_id(0)
    scale = 1.0 / math.sqrt(width)

    @pl.when(step == 0)
    def _():
        own = ko_ref[...]
        own_rows = jnp.transpose(own)
        for r in range(parts):
            cols = kp_ref[r]
            kt_s[r] = jnp.zeros(kt_s.shape[1:], BF16)
            kt_s[r, :full, :prows] = cols
            kt_s[r, :full, prows:] = own
            k_s[r] = jnp.zeros(k_s.shape[1:], BF16)
            k_s[r, :prows, :full] = jnp.transpose(cols)
            k_s[r, prows:, :full] = own_rows
        qf_s[...] = jnp.zeros_like(qf_s)
        gl_s[...] = jnp.zeros_like(gl_s)
        acc_s[...] = jnp.zeros_like(acc_s)

    wv = wv_ref[...]
    wk = wk_ref[...]
    q = q_ref[...]
    ct = ct_ref[...]
    spot = lax.broadcasted_iota(jnp.int32, (tokens, 1), 0)
    live = jnp.zeros((tokens, 1), F32)
    for r in range(parts):
        alive = (spot >= r * rows) & (spot < r * rows + rlen[r])
        live = jnp.where(alive, 1.0, live)
    for j in range(heads):
        wk_j = wk[:, j * nope : (j + 1) * nope]
        wv_j = wv[:, j * val : (j + 1) * val]
        at = j * width
        q_lat = dot(q[:, at : at + nope], wk_j, NT).astype(BF16)
        q_rope = q[:, at + nope : at + width]
        g_lat = (dot(ct[:, j * val : (j + 1) * val], wv_j, NT) * live).astype(BF16)
        for r in range(parts):
            here = slice(r * rows, (r + 1) * rows)
            there = slice(j * rows, (j + 1) * rows)
            qf_s[r, there, :lat] = q_lat[here]
            qf_s[r, there, lat:full] = q_rope[here]
            gl_s[r, there, :lat] = g_lat[here]
    block = heads * rows
    keys = kt_s.shape[2]
    for r in range(parts):
        qf, gl = qf_s[r], gl_s[r]
        scores = dot(qf, kt_s[r]) * scale
        place = lax.broadcasted_iota(jnp.int32, (block, keys), 0) % rows
        key = lax.broadcasted_iota(jnp.int32, (block, keys), 1)
        own = key - (prows + r * rows)
        valid = (key < plen[r]) | ((own >= 0) & (own <= place))
        scores = jnp.where(valid, scores, -jnp.inf)
        expo = jnp.exp(scores - jnp.max(scores, axis=1, keepdims=True))
        weights = expo / jnp.sum(expo, axis=1, keepdims=True)
        weights_bf = weights.astype(BF16)
        lo_s[r] = dot(weights_bf, k_s[r, :, :lat]).astype(BF16)
        grad_w = dot(gl[:, :lat], kt_s[r, :lat])
        inner = jnp.sum(weights * grad_w, axis=1, keepdims=True)
        grad_s = (weights * (grad_w - inner) * scale).astype(BF16)
        gf_s[r] = dot(grad_s, k_s[r]).astype(BF16)
        both = jnp.concatenate([grad_s, weights_bf], axis=0)
        rest = jnp.concatenate([qf, gl], axis=0)
        grad_k = dot(both, rest, TN)
        acc_s[r * prows : (r + 1) * prows] += grad_k[:prows]
        acc_s[parts * prows :] += grad_k[prows:]
    pieces = []
    for j in range(heads):
        wk_j = wk[:, j * nope : (j + 1) * nope]
        wv_j = wv[:, j * val : (j + 1) * val]
        there = slice(j * rows, (j + 1) * rows)
        low = jnp.concatenate([lo_s[r, there] for r in range(parts)], axis=0)
        gf = jnp.concatenate([gf_s[r, there] for r in range(parts)], axis=0)
        out_ref[:, j * val : (j + 1) * val] = (dot(low, wv_j) * live).astype(BF16)
        pieces += [dot(gf[:, :lat], wk_j).astype(BF16), gf[:, lat:full]]
    gq_ref[...] = jnp.concatenate(pieces, axis=1)

    @pl.when(step == pl.num_programs(0) - 1)
    def _():
        gk_ref[...] = jnp.transpose(acc_s[...])[:full].astype(BF16)


def attend(plen, rlen, queries, cotangent, weights, k_prompt, k_own, nope):
    parts, full, prows = k_prompt.shape
    lat = weights.shape[0]
    rope = full - lat
    width = nope + rope
    tokens = queries.shape[0]
    heads = queries.shape[1] // width
    val = cotangent.shape[1] // heads
    rows = tokens // parts
    hs = STEP_HEADS
    steps = heads // hs
    sizes = (parts, rows, hs, nope, rope, val, lat, prows)
    wide = -(-full // 128) * 128
    keys = prows + tokens
    whole = lambda *shape: pl.BlockSpec(shape, lambda i, *_: (0,) * len(shape))
    flops = 2 * tokens * heads * (4 * lat * nope + keys * (3 * full + 3 * lat))
    return pl.pallas_call(
        functools.partial(attend_kernel, sizes),
        out_shape=(
            jax.ShapeDtypeStruct((tokens, heads * val), BF16),
            jax.ShapeDtypeStruct((tokens, heads * width), BF16),
            jax.ShapeDtypeStruct((full, parts * prows + tokens), BF16),
        ),
        grid_spec=pltpu.PrefetchScalarGridSpec(
            num_scalar_prefetch=2,
            grid=(steps,),
            in_specs=[
                pl.BlockSpec((tokens, hs * width), lambda i, *_: (0, i)),
                pl.BlockSpec((tokens, hs * val), lambda i, *_: (0, i)),
                pl.BlockSpec((lat, hs * val), lambda i, *_: (0, i)),
                pl.BlockSpec((lat, hs * nope), lambda i, *_: (0, i + steps)),
                whole(parts, full, prows),
                whole(full, tokens),
            ],
            out_specs=[
                pl.BlockSpec((tokens, hs * val), lambda i, *_: (0, i)),
                pl.BlockSpec((tokens, hs * width), lambda i, *_: (0, i)),
                whole(full, parts * prows + tokens),
            ],
            scratch_shapes=[
                pltpu.VMEM((parts, keys, wide), BF16),
                pltpu.VMEM((parts, wide, keys), BF16),
                pltpu.VMEM((parts, hs * rows, wide), BF16),
                pltpu.VMEM((parts, hs * rows, wide), BF16),
                pltpu.VMEM((parts, hs * rows, lat), BF16),
                pltpu.VMEM((parts, hs * rows, wide), BF16),
                pltpu.VMEM((parts * prows + tokens, wide), F32),
            ],
        ),
        compiler_params=pltpu.CompilerParams(
            dimension_semantics=("arbitrary",), vmem_limit_bytes=48 << 20
        ),
        cost_estimate=pl.CostEstimate(
            flops=flops, transcendentals=tokens * heads * keys, bytes_accessed=8 << 20
        ),
        name="attend",
    )(plen, rlen, queries, cotangent, weights, weights, k_prompt, k_own)


def side_of(axis):
    return math.isqrt(lax.axis_size(axis))


def rows_of(side):
    return [[y * side + z for z in range(side)] for y in range(side)]


def columns_of(side):
    return [[y * side + z for y in range(side)] for z in range(side)]


def exchange(tiles, axis, groups=None):
    return lax.all_to_all(tiles, axis, 0, 0, axis_index_groups=groups, tiled=True)


def to_all(array, count, axis, groups=None):
    return exchange(jnp.broadcast_to(array, (count, *array.shape)), axis, groups)


def body(
    queries,
    resp_latent,
    prompt_latent,
    up_keys,
    up_values,
    cotangent,
    prompt_len,
    resp_len,
    resp_count,
    owner,
):
    head_devices = lax.axis_size("head")
    side = side_of("resp")
    along_z, along_y = rows_of(side), columns_of(side)
    my_index = lax.axis_index("resp")
    my_y, my_z = my_index // side, my_index % side
    head_index = lax.axis_index("head")
    heads, nope, lat_piece = up_keys.shape
    val = up_values.shape[2]
    resp_total = resp_len.shape[0]
    per_device = resp_total // lax.axis_size("resp")
    _, prompt_rows, full = prompt_latent.shape
    share = full // head_devices

    tiles = jnp.concatenate([up_values, jnp.swapaxes(up_keys, 1, 2)], axis=0)
    flat = tiles.reshape(-1, tiles.shape[2])
    weight_rows = flat.shape[0]
    cols = jnp.swapaxes(prompt_latent[0], 0, 1)
    cols = lax.dynamic_slice_in_dim(cols, head_index * share, share, 0)
    got = to_all(jnp.concatenate([flat, cols], axis=0), side, "resp", along_z)
    stripes = got[:, :weight_rows].reshape(side, *tiles.shape)
    stripes = jnp.moveaxis(stripes, 2, 1).reshape(side * lat_piece, -1)
    weights = lax.all_gather(
        stripes, "resp", axis=0, tiled=True, axis_index_groups=along_y
    )
    row_prompts = got[:, weight_rows:]

    starts = jnp.cumsum(resp_count) - resp_count
    numbers = jnp.arange(resp_total, dtype=jnp.int32)
    prompt_of = jnp.sum((starts[None, :] <= numbers[:, None]).astype(jnp.int32), axis=1) - 1
    chosen = prompt_of[:, None] == jnp.arange(prompt_len.shape[0], dtype=jnp.int32)[None, :]
    slot_of = jnp.sum(jnp.where(chosen, owner[None, :], 0), axis=1)
    plen_of = jnp.sum(jnp.where(chosen, prompt_len[None, :], 0), axis=1)
    first = my_index * per_device
    plen_mine = lax.dynamic_slice_in_dim(plen_of, first, per_device)
    rlen_mine = lax.dynamic_slice_in_dim(resp_len, first, per_device)
    slots_mine = lax.dynamic_slice_in_dim(slot_of, first, per_device)

    by_place = slot_of.reshape(side, side, per_device)
    in_column = lax.dynamic_index_in_dim(by_place, my_z, 1, keepdims=False)
    wanted = jnp.take(row_prompts, (in_column % side).reshape(-1), axis=0)
    wanted = wanted.reshape(side, per_device, share, prompt_rows)
    arrived = exchange(wanted, "resp", along_y)
    mine = (slots_mine // side)[None, :] == jnp.arange(side, dtype=jnp.int32)[:, None]
    fetched = jnp.sum(
        jnp.where(mine[:, :, None, None], arrived, 0).astype(F32), axis=0
    ).astype(BF16)
    k_prompt = to_all(fetched, head_devices, "head")
    k_prompt = jnp.moveaxis(k_prompt, 0, 1).reshape(per_device, full, prompt_rows)
    k_own = jnp.swapaxes(resp_latent, 0, 1)

    attended, grad_query, grad_key = attend(
        plen_mine, rlen_mine, queries, cotangent, weights, k_prompt, k_own, nope
    )
    by_head = exchange(grad_key.reshape(head_devices, share, -1), "head")
    summed = jnp.sum(by_head.astype(F32), axis=0)
    split = per_device * prompt_rows
    grad_own = jnp.swapaxes(summed[:, split:], 0, 1)
    grad_prompt = summed[:, :split].astype(BF16)
    in_row = to_all(grad_prompt, side, "resp", along_z)
    row_slots = lax.dynamic_index_in_dim(by_place, my_y, 0, keepdims=False)
    takers = jnp.arange(side, dtype=jnp.int32) * side + my_z
    in_row = in_row.reshape(side, share, per_device, prompt_rows).astype(F32)
    to_owner = []
    for y in range(side):
        ours = row_slots == takers[y]
        kept = jnp.where(ours[:, None, :, None], in_row, 0.0)
        to_owner.append(jnp.sum(kept, axis=(0, 2)).astype(BF16))
    at_owner = exchange(jnp.stack(to_owner), "resp", along_y)
    at_owner = jnp.sum(at_owner.astype(F32), axis=0)
    return (attended, grad_query, grad_own, jnp.swapaxes(at_owner, 0, 1)[None])


def solution(mesh):
    placed = (
        P("resp", "head"),
        P("resp", None),
        P("resp", None, None),
        P("head", None, "resp"),
        P("head", "resp", None),
        P("resp", "head"),
        P(),
        P(),
        P(),
        P(),
    )
    return jax.shard_map(
        body,
        mesh=mesh,
        in_specs=placed,
        out_specs=(
            P("resp", "head"),
            P("resp", "head"),
            P("resp", "head"),
            P("resp", None, "head"),
        ),
        check_vma=False,
    )
```

time: 218 us -> 176 us (0.81)
  blocking collectives: 0 us -> 30 us
  starting transfers between devices: 56.8 us -> 27.6 us
  local copies, waits for them, and re-layouts: 36.1 us -> 13.8 us
  Pallas kernels: 0 us -> 16.5 us
  waiting for transfers between devices: 74.4 us -> 60.2 us
  matrix products: 13.8 us -> 0 us
  other arithmetic: 21.5 us -> 10.6 us
    all_to_all x0 -> x1, blocking collectives: none -> 30 us  [exchange(): lax.all_to_all(tiles, axis, 0, 0, axis_index_groups=groups, tiled=True)]
    all_to_all x7 -> x5, starting transfers between devices: 56.7 us -> 27.6 us  [exchange(): lax.all_to_all(tiles, axis, 0, 0, axis_index_groups=groups, tiled=True)]
    pallas_call x0 -> x1, Pallas kernels: none -> 16.5 us  [attend(): pl.pallas_call(functools.partial(attend_kernel, sizes), out_shape=(jax.Sh...]
    slice x15 -> x3, local copies, waits for them, and re-layouts: 15.9 us -> 0.7 us  [the longest x1 0.68 us: body(): ours = row_slots == takers[y]]
    sub x1 -> x0, other arithmetic: 11.3 us -> none  [attend(): grad_weights - inner]
    all_gather x1, waiting for transfers between devices: 26.7 us -> 18.9 us  [body(): lax.all_gather(stripes, 'resp', axis=0, tiled=True, axis_index_groups=alo...]
    all_to_all x7 -> x5, waiting for transfers between devices: 47.7 us -> 41.4 us  [exchange(): lax.all_to_all(tiles, axis, 0, 0, axis_index_groups=groups, tiled=True)]
    sub x1 -> x0, matrix products: 5.22 us -> none  [attend(): expo = jnp.exp(scores - row_max)]
  transfers between devices with their start and end apart: 8 -> 6, of which waited for: 8 -> 6; matrix products, arithmetic and copies ran while one was open for 9% -> 8% of each run, Pallas kernels for 0% -> 0%
where the time goes in v1:
time: 176 us; the launch traced here: 173 us
  waiting for transfers between devices  60.2 us (34%)
  blocking collectives  30 us (17%)
  starting transfers between devices  27.6 us (16%)
  Pallas kernels  16.5 us (9%)
  between operations  14.3 us (8%)
  local copies, waits for them, and re-layouts  13.8 us (8%)
  other arithmetic  10.6 us (6%)
    all_to_all x5, waiting for transfers between devices, exchange(): lax.all_to_all(tiles, axis, 0, 0, axis_index_groups=groups, tiled=True)  41.4 us
    all_to_all x1, blocking collectives, exchange(): lax.all_to_all(tiles, axis, 0, 0, axis_index_groups=groups, tiled=True)  30 us
    all_to_all x5, starting transfers between devices, exchange(): lax.all_to_all(tiles, axis, 0, 0, axis_index_groups=groups, tiled=True)  27.6 us
    all_gather x1, waiting for transfers between devices, body(): lax.all_gather(stripes, 'resp', axis=0, tiled=True, axis_index_groups=alo...  18.9 us
    pallas_call x1, Pallas kernels, attend(): pl.pallas_call(functools.partial(attend_kernel, sizes), out_shape=(jax.Sh...  16.5 us
    unnamed x17, local copies, waits for them, and re-layouts  5.05 us
    eq x1, other arithmetic, body(): ours = row_slots == takers[y]  5.04 us
  transfers between devices with their start and end apart: 6, of which 6 were waited for; matrix products, arithmetic and copies ran while one was open for 8% of the time, Pallas kernels for 0%

profile of v1, /device:TPU:1, one launch (start us, length us, event | category | flops | bytes accessed | tf_op | source)
XLA Modules:
  0.0 173.1 jit_solution(11547570457222104240)
XLA Ops:
  7.3 0.8 copy-done
  8.1 0.8 maximum_bitcast_fusion
  9.0 30.0 %all_to_all.30 = bf16[8,328,128]{2,1,0:T(8,128)(2,1)S(1)} all-to-all(bf16[8,328,128]{2,1,0:T(8,128)(2,1)S(1)} %broadcast_in_dim.157), channel_id=1, replica_groups={{0,8,16,24,32,40,48,56},{64,72,80,88,96,104,112,120},{128,136,144,152,1..., dimensions={0} | all-to-all | bytes 1343488 | tf_op jit(solution)/shard_map/all_to_all | solution.py:181
  38.9 0.8 slice_bitcast_fusion
  39.8 0.7 copy.49
  40.6 0.1 reduce.17
  40.7 0.7 sub.15
  41.5 0.8 select_reduce_fusion.1
  42.2 0.1 reshape.295
  42.4 0.5 broadcast.229
  42.9 0.7 fusion.11
  43.7 0.1 copy.51
  43.9 0.6 gather_fusion
  44.5 0.8 broadcast_select_fusion
  45.3 6.8 %all-to-all-start.1 = ((bf16[8,2,72,128]{3,2,1,0:T(8,128)(2,1)}), bf16[8,2,72,128]{3,2,1,0:T(8,128)(2,1)S(1)}, u32[]{:S(2)}, u32[]{:S(2)}) async-start(bf16[8,2,72,128]{3,2,1,0:T(8,128)(2,1)} %broadcast_select_fusion), calls=%async_computation.1 | async-start | bytes 589824 | tf_op jit(solution)/shard_map/all_to_all | solution.py:181
  52.2 14.7 %all-to-all-done.1 = bf16[8,2,72,128]{3,2,1,0:T(8,128)(2,1)S(1)} async-done(((bf16[8,2,72,128]{3,2,1,0:T(8,128)(2,1)}), bf16[8,2,72,128]{3,2,1,0:T(8,128)(2,1)S(1)}, u32[]{:S(2)}, u32[]{:S(2)}) %all-to-all-start.1) | async-done | bytes 294944 | tf_op jit(solution)/shard_map/all_to_all | solution.py:181
  67.0 0.1 select_reduce_fusion
  67.1 0.8 broadcast_in_dim.163
  67.8 7.4 %all-to-all-start.2 = ((bf16[8,2,72,128]{3,2,1,0:T(8,128)(2,1)}), bf16[8,2,72,128]{3,2,1,0:T(8,128)(2,1)S(1)}, u32[]{:S(2)}, u32[]{:S(2)}) async-start(bf16[8,2,72,128]{3,2,1,0:T(8,128)(2,1)} %broadcast_in_dim.163), calls=%async_computation.2 | async-start | bytes 589824 | tf_op jit(solution)/shard_map/all_to_all | solution.py:181
  75.4 6.7 %all-to-all-done.2 = bf16[8,2,72,128]{3,2,1,0:T(8,128)(2,1)S(1)} async-done(((bf16[8,2,72,128]{3,2,1,0:T(8,128)(2,1)}), bf16[8,2,72,128]{3,2,1,0:T(8,128)(2,1)S(1)}, u32[]{:S(2)}, u32[]{:S(2)}) %all-to-all-start.2) | async-done | bytes 294944 | tf_op jit(solution)/shard_map/all_to_all | solution.py:181
  82.2 18.9 %all-gather.2.cloned.1.call-done.wv_ref.wk_ref = bf16[512,4096]{1,0:T(8,128)(2,1)} async-done(((bf16[64,4096]{1,0:T(8,128)(2,1)}), bf16[512,4096]{1,0:T(8,128)(2,1)}) %all-gather.2.cloned.1.call-update) | async-done | bytes 4194320 | tf_op jit(solution)/shard_map/all_gather | solution.py:221
  101.0 16.5 %attend.1 = (bf16[128,2048]{1,0:T(8,128)(2,1)}, bf16[128,3072]{1,0:T(8,128)(2,1)}, bf16[576,384]{1,0:T(8,128)(2,1)}) custom-call(s32[2]{0:T(128)S(1)} %dynamic_slice.20.plen, s32[2]{0:T(128)S(1)} %dynamic_slice.21.rlen, bf16[128,3072]{1,0:T(8,128)(2,1)S(1)} %copy-done.1, bf16[128,2048]{1,0:T(8,128)(2,1)S(1)} %copy-done.2, ...), custom_call_target="tpu_custom_call" | custom-call | flops 4496293888 | bytes 8388608 | tf_op jit(solution)/shard_map/attend/pallas_call | solution.py:125
  117.6 5.1 %all-to-all-start.3 = ((bf16[8,72,384]{2,1,0:T(8,128)(2,1)}), bf16[8,72,384]{2,1,0:T(8,128)(2,1)S(1)}, u32[]{:S(2)}, u32[]{:S(2)}) async-start(bf16[8,72,384]{2,1,0:T(8,128)(2,1)} %bitcast.14), calls=%async_computation.3 | async-start | bytes 884736 | tf_op jit(solution)/shard_map/all_to_all | solution.py:181
  122.7 0.7 fusion.12
  123.3 5.0 %broadcast_compare_fusion.7 = (pred[1,8,2]{2,1,0:T(8,128)(4,1)S(1)}, pred[1,8,2]{2,1,0:T(8,128)(4,1)S(1)}, pred[1,8,2]{2,1,0:T(8,128)(4,1)S(1)}, pred[1,8,2]{2,1...) fusion(s32[]{:T(128)} %bitcast.16, ...), kind=kLoop, calls=%fused_computation.63 | loop fusion | flops 128 | bytes 228 | tf_op jit(solution)/shard_map/eq | solution.py:264
  128.4 0.1 copy.61
  128.9 2.3 %all-to-all-done.3 = bf16[8,72,384]{2,1,0:T(8,128)(2,1)S(1)} async-done(((bf16[8,72,384]{2,1,0:T(8,128)(2,1)}), bf16[8,72,384]{2,1,0:T(8,128)(2,1)S(1)}, u32[]{:S(2)}, u32[]{:S(2)}) %all-to-all-start.3) | async-done | bytes 442400 | tf_op jit(solution)/shard_map/all_to_all | solution.py:181
  131.2 0.7 broadcast_in_dim.167
  131.9 4.0 %all-to-all-start.4 = ((bf16[8,72,256]{2,1,0:T(8,128)(2,1)}), bf16[8,72,256]{2,1,0:T(8,128)(2,1)S(1)}, u32[]{:S(2)}, u32[]{:S(2)}) async-start(bf16[8,72,256]{2,1,0:T(8,128)(2,1)} %broadcast_in_dim.167), calls=%async_computation.4 | async-start | bytes 589824 | tf_op jit(solution)/shard_map/all_to_all | solution.py:181
  136.5 10.2 %all-to-all-done.4 = bf16[8,72,256]{2,1,0:T(8,128)(2,1)S(1)} async-done(((bf16[8,72,256]{2,1,0:T(8,128)(2,1)}), bf16[8,72,256]{2,1,0:T(8,128)(2,1)S(1)}, u32[]{:S(2)}, u32[]{:S(2)}) %all-to-all-start.4) | async-done | bytes 294944 | tf_op jit(solution)/shard_map/all_to_all | solution.py:181
  146.7 0.6 fusion.7
  147.5 0.1 reduce_sum.195
  147.6 0.1 reduce_sum.198
  147.8 0.1 reduce_sum.201
  147.9 0.1 reduce_sum.204
  148.1 0.1 reduce_sum.207
  148.4 0.6 bitcast_dynamic-update-slice_fusion.7
  149.0 0.6 bitcast_dynamic-update-slice_fusion.6
  149.6 0.6 bitcast_dynamic-update-slice_fusion.5
  150.2 0.6 bitcast_dynamic-update-slice_fusion.4
  150.9 0.6 bitcast_dynamic-update-slice_fusion.3
  151.5 0.6 bitcast_dynamic-update-slice_fusion.2
  152.1 0.6 bitcast_dynamic-update-slice_fusion.1
  152.7 0.6 bitcast_dynamic-update-slice_fusion
  153.3 4.3 %all-to-all-start.5 = ((bf16[8,72,128]{2,1,0:T(8,128)(2,1)}), bf16[8,72,128]{2,1,0:T(8,128)(2,1)S(1)}, u32[]{:S(2)}, u32[]{:S(2)}) async-start(bf16[8,72,128]{2,1,0:T(8,128)(2,1)} %bitcast_dynamic-update-slice_fusion), calls=%async_computation.5 | async-start | bytes 294912 | tf_op jit(solution)/shard_map/all_to_all | solution.py:181
  157.5 0.6 slice_bitcast_fusion.1
  158.1 7.5 %all-to-all-done.5 = bf16[8,72,128]{2,1,0:T(8,128)(2,1)S(1)} async-done(((bf16[8,72,128]{2,1,0:T(8,128)(2,1)}), bf16[8,72,128]{2,1,0:T(8,128)(2,1)S(1)}, u32[]{:S(2)}, u32[]{:S(2)}) %all-to-all-start.5) | async-done | bytes 147488 | tf_op jit(solution)/shard_map/all_to_all | solution.py:181
  165.6 0.6 convert_reduce_fusion.1
  (53 shorter events, 2.5 us)
Async XLA Ops:
  7.2 0.9 copy-start
  7.2 68.1 %copy-start.4 = (s32[128]{0:T(128)S(1)}, s32[128]{0:T(128)}, u32[]{:S(2)}) copy-start(s32[128]{0:T(128)} %param.17) | copy-start | bytes 1540
  7.2 93.8 %copy-start.2 = (bf16[128,2048]{1,0:T(8,128)(2,1)S(1)}, bf16[128,2048]{1,0:T(8,128)(2,1)}, u32[]{:S(2)}) copy-start(bf16[128,2048]{1,0:T(8,128)(2,1)} %ct_ref.1) | copy-start | bytes 1572868
  7.2 93.8 %copy-start.3 = (bf16[128,576]{0,1:T(8,128)(2,1)S(1)}, bf16[128,576]{0,1:T(8,128)(2,1)}, u32[]{:S(2)}) copy-start(bf16[128,576]{0,1:T(8,128)(2,1)} %param.11) | copy-start | bytes 442372
  7.2 93.8 %copy-start.1 = (bf16[128,3072]{1,0:T(8,128)(2,1)S(1)}, bf16[128,3072]{1,0:T(8,128)(2,1)}, u32[]{:S(2)}) copy-start(bf16[128,3072]{1,0:T(8,128)(2,1)} %q_ref.1) | copy-start | bytes 2359300
  7.2 93.8 %all-gather.2.cloned.1.call-start = ((), (), s32[]{:S(2)}) async-start(), calls=%async_computation.6 | async-start | bytes 4718592 | tf_op jit(solution)/shard_map/all_gather | solution.py:221
  45.3 21.6 %all-to-all-start.1 = ((bf16[8,2,72,128]{3,2,1,0:T(8,128)(2,1)}), bf16[8,2,72,128]{3,2,1,0:T(8,128)(2,1)S(1)}, u32[]{:S(2)}, u32[]{:S(2)}) async-start(bf16[8,2,72,128]{3,2,1,0:T(8,128)(2,1)} %broadcast_select_fusion), calls=%async_computation.1 | async-start | bytes 589824 | tf_op jit(solution)/shard_map/all_to_all | solution.py:181
  67.8 14.3 %all-to-all-start.2 = ((bf16[8,2,72,128]{3,2,1,0:T(8,128)(2,1)}), bf16[8,2,72,128]{3,2,1,0:T(8,128)(2,1)S(1)}, u32[]{:S(2)}, u32[]{:S(2)}) async-start(bf16[8,2,72,128]{3,2,1,0:T(8,128)(2,1)} %broadcast_in_dim.163), calls=%async_computation.2 | async-start | bytes 589824 | tf_op jit(solution)/shard_map/all_to_all | solution.py:181
  117.6 13.6 %all-to-all-start.3 = ((bf16[8,72,384]{2,1,0:T(8,128)(2,1)}), bf16[8,72,384]{2,1,0:T(8,128)(2,1)S(1)}, u32[]{:S(2)}, u32[]{:S(2)}) async-start(bf16[8,72,384]{2,1,0:T(8,128)(2,1)} %bitcast.14), calls=%async_computation.3 | async-start | bytes 884736 | tf_op jit(solution)/shard_map/all_to_all | solution.py:181
  131.9 14.8 %all-to-all-start.4 = ((bf16[8,72,256]{2,1,0:T(8,128)(2,1)}), bf16[8,72,256]{2,1,0:T(8,128)(2,1)S(1)}, u32[]{:S(2)}, u32[]{:S(2)}) async-start(bf16[8,72,256]{2,1,0:T(8,128)(2,1)} %broadcast_in_dim.167), calls=%async_computation.4 | async-start | bytes 589824 | tf_op jit(solution)/shard_map/all_to_all | solution.py:181
  153.3 12.4 %all-to-all-start.5 = ((bf16[8,72,128]{2,1,0:T(8,128)(2,1)}), bf16[8,72,128]{2,1,0:T(8,128)(2,1)S(1)}, u32[]{:S(2)}, u32[]{:S(2)}) async-start(bf16[8,72,128]{2,1,0:T(8,128)(2,1)} %bitcast_dynamic-update-slice_fusion), calls=%async_computation.5 | async-start | bytes 294912 | tf_op jit(solution)/shard_map/all_to_all | solution.py:181
Sparse Core Ops, SparseCore 0:
  39.9 61.0 all-gather.1

commit v2 on v1

v2 whole, which is shorter than its diff:
```python
import functools
import math

import jax
import jax.numpy as jnp
from jax import lax
from jax.experimental import pallas as pl
from jax.experimental.pallas import tpu as pltpu
from jax.sharding import PartitionSpec as P

F32, BF16 = jnp.float32, jnp.bfloat16
STEP_HEADS = 4
NT, TN = ((1,), (1,)), ((0,), (0,))


def dot(left, right, dims=((1,), (0,))):
    return lax.dot_general(left, right, (dims, ((), ())), preferred_element_type=F32)


def whole(*shape):
    return pl.BlockSpec(shape, lambda i, *_: (0,) * len(shape))


def keys_kernel(kp_ref, ko_ref, k_ref, kt_ref):
    parts, full, prows = kp_ref.shape
    own = ko_ref[...]
    own_rows = jnp.transpose(own)
    for r in range(parts):
        cols = kp_ref[r]
        kt_ref[r] = jnp.zeros(kt_ref.shape[1:], BF16)
        kt_ref[r, :full, :prows] = cols
        kt_ref[r, :full, prows:] = own
        k_ref[r] = jnp.zeros(k_ref.shape[1:], BF16)
        k_ref[r, :prows, :full] = jnp.transpose(cols)
        k_ref[r, prows:, :full] = own_rows


def both_keys(k_prompt, k_own):
    parts, full, prows = k_prompt.shape
    keys = prows + k_own.shape[1]
    wide = -(-full // 128) * 128
    shapes = (parts, keys, wide), (parts, wide, keys)
    return pl.pallas_call(
        keys_kernel,
        out_shape=tuple(jax.ShapeDtypeStruct(s, BF16) for s in shapes),
        grid=(1,),
        in_specs=[whole(*k_prompt.shape), whole(*k_own.shape)],
        out_specs=[whole(*s) for s in shapes],
        compiler_params=pltpu.CompilerParams(vmem_limit_bytes=12 << 20),
        name="both_keys",
    )(k_prompt, k_own)


def live_rows(rlen, parts, rows):
    spot = lax.broadcasted_iota(jnp.int32, (parts * rows, 1), 0)
    live = jnp.zeros(spot.shape, F32)
    for r in range(parts):
        alive = (spot >= r * rows) & (spot < r * rows + rlen[r])
        live = jnp.where(alive, 1.0, live)
    return live


def scores_kernel(
    sizes, plen, rlen, q_ref, ct_ref, wv_ref, wk_ref, kt_ref,
    gk_ref, w_ref, gs_ref, qf_s, gl_s, acc_s,
):
    parts, rows, heads, nope, rope, val, lat, prows = sizes
    full, width = lat + rope, nope + rope
    step = pl.program_id(0)
    scale = 1.0 / math.sqrt(width)

    @pl.when(step == 0)
    def _():
        qf_s[...] = jnp.zeros_like(qf_s)
        gl_s[...] = jnp.zeros_like(gl_s)
        acc_s[...] = jnp.zeros_like(acc_s)

    wv, wk, q, ct = wv_ref[...], wk_ref[...], q_ref[...], ct_ref[...]
    live = live_rows(rlen, parts, rows)
    for j in range(heads):
        at = j * width
        q_lat = dot(q[:, at : at + nope], wk[:, j * nope : (j + 1) * nope], NT).astype(BF16)
        q_rope = q[:, at + nope : at + width]
        heard = dot(ct[:, j * val : (j + 1) * val], wv[:, j * val : (j + 1) * val], NT)
        g_lat = (heard * live).astype(BF16)
        for r in range(parts):
            here = slice(r * rows, (r + 1) * rows)
            there = slice(j * rows, (j + 1) * rows)
            qf_s[r, there, :lat] = q_lat[here]
            qf_s[r, there, lat:full] = q_rope[here]
            gl_s[r, there, :lat] = g_lat[here]
    block, keys = heads * rows, kt_ref.shape[2]
    for r in range(parts):
        qf, gl = qf_s[r], gl_s[r]
        scores = dot(qf, kt_ref[r]) * scale
        place = lax.broadcasted_iota(jnp.int32, (block, keys), 0) % rows
        key = lax.broadcasted_iota(jnp.int32, (block, keys), 1)
        own = key - (prows + r * rows)
        valid = (key < plen[r]) | ((own >= 0) & (own <= place))
        scores = jnp.where(valid, scores, -jnp.inf)
        expo = jnp.exp(scores - jnp.max(scores, axis=1, keepdims=True))
        weights = expo / jnp.sum(expo, axis=1, keepdims=True)
        weights_bf = weights.astype(BF16)
        grad_w = dot(gl[:, :lat], kt_ref[r, :lat])
        inner = jnp.sum(weights * grad_w, axis=1, keepdims=True)
        grad_s = (weights * (grad_w - inner) * scale).astype(BF16)
        w_ref[r] = weights_bf
        gs_ref[r] = grad_s
        both = jnp.concatenate([grad_s, weights_bf], axis=0)
        rest = jnp.concatenate([qf, gl], axis=0)
        grad_k = dot(both, rest, TN)
        acc_s[r * prows : (r + 1) * prows] += grad_k[:prows]
        acc_s[parts * prows :] += grad_k[prows:]

    @pl.when(step == pl.num_programs(0) - 1)
    def _():
        gk_ref[...] = jnp.transpose(acc_s[...])[:full].astype(BF16)


def values_kernel(sizes, rlen, wv_ref, wk_ref, k_ref, w_ref, gs_ref, out_ref, gq_ref):
    parts, rows, heads, nope, rope, val, lat, prows = sizes
    full = lat + rope
    wv, wk = wv_ref[...], wk_ref[...]
    live = live_rows(rlen, parts, rows)
    lows = [dot(w_ref[r], k_ref[r, :, :lat]).astype(BF16) for r in range(parts)]
    grads = [dot(gs_ref[r], k_ref[r]).astype(BF16) for r in range(parts)]
    pieces = []
    for j in range(heads):
        there = slice(j * rows, (j + 1) * rows)
        low = jnp.concatenate([one[there] for one in lows], axis=0)
        grad = jnp.concatenate([one[there] for one in grads], axis=0)
        heard = dot(low, wv[:, j * val : (j + 1) * val]) * live
        out_ref[:, j * val : (j + 1) * val] = heard.astype(BF16)
        pieces.append(dot(grad[:, :lat], wk[:, j * nope : (j + 1) * nope]).astype(BF16))
        pieces.append(grad[:, lat:full])
    gq_ref[...] = jnp.concatenate(pieces, axis=1)


def attend(plen, rlen, queries, cotangent, weights, k, kt, full, prows, nope):
    parts, keys, wide = k.shape
    lat = weights.shape[0]
    rope = full - lat
    width = nope + rope
    tokens = queries.shape[0]
    heads = queries.shape[1] // width
    val = cotangent.shape[1] // heads
    rows = tokens // parts
    hs = STEP_HEADS
    steps = heads // hs
    sizes = (parts, rows, hs, nope, rope, val, lat, prows)
    wv_spec = pl.BlockSpec((lat, hs * val), lambda i, *_: (0, i))
    wk_spec = pl.BlockSpec((lat, hs * nope), lambda i, *_: (0, i + steps))
    q_spec = pl.BlockSpec((tokens, hs * width), lambda i, *_: (0, i))
    v_spec = pl.BlockSpec((tokens, hs * val), lambda i, *_: (0, i))
    w_spec = pl.BlockSpec((parts, hs * rows, keys), lambda i, *_: (0, i, 0))
    w_shape = jax.ShapeDtypeStruct((parts, heads * rows, keys), BF16)
    params = pltpu.CompilerParams(
        dimension_semantics=("arbitrary",), vmem_limit_bytes=30 << 20
    )
    queries, cotangent, weights, k, kt = (
        pltpu.with_memory_space_constraint(a, pltpu.HBM)
        for a in (queries, cotangent, weights, k, kt)
    )
    grad_key, soft, grad_s = pl.pallas_call(
        functools.partial(scores_kernel, sizes),
        out_shape=(
            jax.ShapeDtypeStruct((full, parts * prows + tokens), BF16),
            w_shape,
            w_shape,
        ),
        grid_spec=pltpu.PrefetchScalarGridSpec(
            num_scalar_prefetch=2,
            grid=(steps,),
            in_specs=[q_spec, v_spec, wv_spec, wk_spec, whole(*kt.shape)],
            out_specs=[whole(full, parts * prows + tokens), w_spec, w_spec],
            scratch_shapes=[
                pltpu.VMEM((parts, hs * rows, wide), BF16),
                pltpu.VMEM((parts, hs * rows, wide), BF16),
                pltpu.VMEM((parts * prows + tokens, wide), F32),
            ],
        ),
        compiler_params=params,
        cost_estimate=pl.CostEstimate(
            flops=2 * tokens * heads * (2 * lat * nope + keys * (2 * full + 2 * lat)),
            transcendentals=tokens * heads * keys,
            bytes_accessed=8 << 20,
        ),
        name="scores",
    )(plen, rlen, queries, cotangent, weights, weights, kt)
    attended, grad_query = pl.pallas_call(
        functools.partial(values_kernel, sizes),
        out_shape=(
            jax.ShapeDtypeStruct((tokens, heads * val), BF16),
            jax.ShapeDtypeStruct((tokens, heads * width), BF16),
        ),
        grid_spec=pltpu.PrefetchScalarGridSpec(
            num_scalar_prefetch=1,
            grid=(steps,),
            in_specs=[wv_spec, wk_spec, whole(*k.shape), w_spec, w_spec],
            out_specs=[v_spec, q_spec],
        ),
        compiler_params=params,
        cost_estimate=pl.CostEstimate(
            flops=2 * tokens * heads * (2 * lat * nope + keys * (full + lat)),
            transcendentals=0,
            bytes_accessed=8 << 20,
        ),
        name="values",
    )(rlen, weights, weights, k, soft, grad_s)
    return attended, grad_query, grad_key


def slots_kernel(place, in_ref, out_ref, acc_s):
    senders, _, wide = in_ref.shape
    takers, _, lanes = out_ref.shape
    parts = wide // lanes
    acc_s[...] = jnp.zeros_like(acc_s)
    for s in range(senders):
        for r in range(parts):
            to = place[s * parts + r]
            acc_s[to] += in_ref[s, :, r * lanes : (r + 1) * lanes].astype(F32)
    out_ref[...] = acc_s[:takers].astype(BF16)


def by_slot(place, in_row, takers, lanes):
    shape = (takers, in_row.shape[1], lanes)
    return pl.pallas_call(
        slots_kernel,
        out_shape=jax.ShapeDtypeStruct(shape, BF16),
        grid_spec=pltpu.PrefetchScalarGridSpec(
            num_scalar_prefetch=1,
            grid=(1,),
            in_specs=[whole(*in_row.shape)],
            out_specs=whole(*shape),
            scratch_shapes=[pltpu.VMEM((takers + 1, *shape[1:]), F32)],
        ),
        compiler_params=pltpu.CompilerParams(vmem_limit_bytes=8 << 20),
        name="by_slot",
    )(place, in_row)


def side_of(axis):
    return math.isqrt(lax.axis_size(axis))


def rows_of(side):
    return [[y * side + z for z in range(side)] for y in range(side)]


def columns_of(side):
    return [[y * side + z for y in range(side)] for z in range(side)]


def exchange(tiles, axis, groups=None):
    return lax.all_to_all(tiles, axis, 0, 0, axis_index_groups=groups, tiled=True)


def to_all(array, count, axis, groups=None):
    return exchange(jnp.broadcast_to(array, (count, *array.shape)), axis, groups)


def body(
    queries,
    resp_latent,
    prompt_latent,
    up_keys,
    up_values,
    cotangent,
    prompt_len,
    resp_len,
    resp_count,
    owner,
):
    head_devices = lax.axis_size("head")
    side = side_of("resp")
    along_z, along_y = rows_of(side), columns_of(side)
    my_index = lax.axis_index("resp")
    my_y, my_z = my_index // side, my_index % side
    head_index = lax.axis_index("head")
    heads, nope, lat_piece = up_keys.shape
    val = up_values.shape[2]
    resp_total = resp_len.shape[0]
    per_device = resp_total // lax.axis_size("resp")
    _, prompt_rows, full = prompt_latent.shape
    share = full // head_devices

    tiles = jnp.concatenate([up_values, jnp.swapaxes(up_keys, 1, 2)], axis=0)
    got = to_all(tiles, side, "resp", along_z)
    stripes = jnp.moveaxis(got, 2, 1).reshape(side * lat_piece, -1)
    weights = lax.all_gather(
        stripes, "resp", axis=0, tiled=True, axis_index_groups=along_y
    )
    cols = jnp.swapaxes(prompt_latent[0], 0, 1)
    cols = lax.dynamic_slice_in_dim(cols, head_index * share, share, 0)
    cols, _ = lax.optimization_barrier((cols, got[0, 0, 0]))
    column_prompts = to_all(cols, side, "resp", along_y)

    starts = jnp.cumsum(resp_count) - resp_count
    numbers = jnp.arange(resp_total, dtype=jnp.int32)
    prompt_of = jnp.sum((starts[None, :] <= numbers[:, None]).astype(jnp.int32), axis=1) - 1
    chosen = prompt_of[:, None] == jnp.arange(prompt_len.shape[0], dtype=jnp.int32)[None, :]
    slot_of = jnp.sum(jnp.where(chosen, owner[None, :], 0), axis=1)
    plen_of = jnp.sum(jnp.where(chosen, prompt_len[None, :], 0), axis=1)
    first = my_index * per_device
    plen_mine = lax.dynamic_slice_in_dim(plen_of, first, per_device)
    rlen_mine = lax.dynamic_slice_in_dim(resp_len, first, per_device)
    slots_mine = lax.dynamic_slice_in_dim(slot_of, first, per_device)

    by_place = slot_of.reshape(side, side, per_device)
    row_slots = lax.dynamic_index_in_dim(by_place, my_y, 0, keepdims=False)
    wanted = jnp.take(column_prompts, (row_slots // side).reshape(-1), axis=0)
    wanted = wanted.reshape(side, per_device, share, prompt_rows)
    arrived = exchange(wanted, "resp", along_z)
    mine = (slots_mine % side)[None, :] == jnp.arange(side, dtype=jnp.int32)[:, None]
    fetched = jnp.sum(
        jnp.where(mine[:, :, None, None], arrived, 0).astype(F32), axis=0
    ).astype(BF16)
    k_prompt = to_all(fetched, head_devices, "head")
    k_prompt = jnp.moveaxis(k_prompt, 0, 1).reshape(per_device, full, prompt_rows)
    k_own = jnp.swapaxes(resp_latent, 0, 1)

    k, kt = both_keys(k_prompt, k_own)

    attended, grad_query, grad_key = attend(
        plen_mine, rlen_mine, queries, cotangent, weights, k, kt, full, prompt_rows, nope
    )
    by_head = exchange(grad_key.reshape(head_devices, share, -1), "head")
    summed = jnp.sum(by_head.astype(F32), axis=0)
    split = per_device * prompt_rows
    grad_own = jnp.swapaxes(summed[:, split:], 0, 1)
    grad_prompt = summed[:, :split].astype(BF16)
    in_row = to_all(grad_prompt, side, "resp", along_z)
    place = jnp.where(row_slots % side == my_z, row_slots // side, side).reshape(-1)
    to_owner = by_slot(place, in_row, side, prompt_rows)
    at_owner = exchange(to_owner, "resp", along_y)
    at_owner = jnp.sum(at_owner.astype(F32), axis=0)
    return (attended, grad_query, grad_own, jnp.swapaxes(at_owner, 0, 1)[None])


def solution(mesh):
    placed = (
        P("resp", "head"),
        P("resp", None),
        P("resp", None, None),
        P("head", None, "resp"),
        P("head", "resp", None),
        P("resp", "head"),
        P(),
        P(),
        P(),
        P(),
    )
    return jax.shard_map(
        body,
        mesh=mesh,
        in_specs=placed,
        out_specs=(
            P("resp", "head"),
            P("resp", "head"),
            P("resp", "head"),
            P("resp", None, "head"),
        ),
        check_vma=False,
    )
```

time: 176 us -> 157 us (0.89)
  waiting for transfers between devices: 60.2 us -> 39.8 us
  blocking collectives: 30 us -> 40.2 us
  local copies, waits for them, and re-layouts: 13.8 us -> 6.55 us
  other arithmetic: 10.6 us -> 4.33 us
  Pallas kernels: 16.5 us -> 19.6 us
  starting transfers between devices: 27.6 us -> 29.9 us
    all_gather x1, waiting for transfers between devices: 18.9 us -> 6.55 us  [body(): lax.all_gather(stripes, 'resp', axis=0, tiled=True, axis_index_groups=alo...]
    all_to_all x1 -> x2, blocking collectives: 30 us -> 40.2 us  [exchange(): lax.all_to_all(tiles, axis, 0, 0, axis_index_groups=groups, tiled=True)]
    all_to_all x5, waiting for transfers between devices: 41.4 us -> 33.2 us  [exchange(): lax.all_to_all(tiles, axis, 0, 0, axis_index_groups=groups, tiled=True)]
    eq x2 -> x1, other arithmetic: 5.05 us -> 0.01 us  [body(): (slots_mine % side)[None, :] == jnp.arange(side, dtype=jnp.int32)[:, None]]
    unnamed x17 -> x10, local copies, waits for them, and re-layouts: 5.05 us -> 1.69 us
    pallas_call x1 -> x4, Pallas kernels: 16.5 us -> 19.6 us  [the longest x1 11.3 us: attend(): pl.pallas_call(functools.partial(scores_kernel, sizes), out_shape=(jax.Sh...]
    all_to_all x5, starting transfers between devices: 27.6 us -> 29.8 us  [exchange(): lax.all_to_all(tiles, axis, 0, 0, axis_index_groups=groups, tiled=True)]
  transfers between devices with their start and end apart: 6 -> 6, of which waited for: 6 -> 6; matrix products, arithmetic and copies ran while one was open for 8% -> 4% of each run, Pallas kernels for 0% -> 5%
where the time goes in v2:
time: 157 us; the launch traced here: 155 us
  blocking collectives  40.2 us (26%)
  waiting for transfers between devices  39.8 us (25%)
  starting transfers between devices  29.9 us (19%)
  Pallas kernels  19.6 us (12%)
  between operations  14.2 us (9%)
  local copies, waits for them, and re-layouts  6.55 us (4%)
  other arithmetic  4.33 us (3%)
    all_to_all x2, blocking collectives, exchange(): lax.all_to_all(tiles, axis, 0, 0, axis_index_groups=groups, tiled=True)  40.2 us
    all_to_all x5, waiting for transfers between devices, exchange(): lax.all_to_all(tiles, axis, 0, 0, axis_index_groups=groups, tiled=True)  33.2 us
    all_to_all x5, starting transfers between devices, exchange(): lax.all_to_all(tiles, axis, 0, 0, axis_index_groups=groups, tiled=True)  29.8 us
    pallas_call x1, Pallas kernels, attend(): pl.pallas_call(functools.partial(scores_kernel, sizes), out_shape=(jax.Sh...  11.3 us
    pallas_call x1, Pallas kernels, attend(): pl.pallas_call(functools.partial(values_kernel, sizes), out_shape=(jax.Sh...  6.68 us
    all_gather x1, waiting for transfers between devices, body(): lax.all_gather(stripes, 'resp', axis=0, tiled=True, axis_index_groups=alo...  6.55 us
  transfers between devices with their start and end apart: 6, of which 6 were waited for; matrix products, arithmetic and copies ran while one was open for 4% of the time, Pallas kernels for 5%

profile of v2, /device:TPU:1, one launch (start us, length us, event | category | flops | bytes accessed | tf_op | source)
XLA Modules:
  0.0 154.5 jit_solution(13069280795857377570)
XLA Ops:
  7.2 0.0 copy-start
  7.2 0.0 all-gather.2.cloned.1.call-start
  7.2 0.9 pad_maximum_fusion
  8.1 0.1 broadcast_in_dim.66
  8.2 26.9 %all_to_all.35 = bf16[8,32,8,128]{3,2,1,0:T(8,128)(2,1)} all-to-all(bf16[8,32,8,128]{3,2,1,0:T(8,128)(2,1)S(1)} %broadcast_in_dim.66), channel_id=1, replica_groups={{0,8,16,24,32,40,48,56},{64,72,80,88,96,104,112,120},{128,136,144,152,1..., dimensions={0} | all-to-all | bytes 1048576 | tf_op jit(solution)/shard_map/all_to_all | solution.py:255
  35.1 0.0 all-gather.2.cloned.1.call-update
  35.1 0.0 copy-done
  35.1 0.7 broadcast_in_dim.71
  35.8 6.8 %all-to-all-start.1 = ((bf16[8,72,128]{2,1,0:T(8,128)(2,1)}), bf16[8,72,128]{2,1,0:T(8,128)(2,1)S(1)}, u32[]{:S(2)}, u32[]{:S(2)}) async-start(bf16[8,72,128]{2,1,0:T(8,128)(2,1)} %broadcast_in_dim.71), calls=%async_computation.1 | async-start | bytes 294912 | tf_op jit(solution)/shard_map/all_to_all | solution.py:255
  42.6 0.7 copy.24
  43.4 0.1 reduce-window.9
  43.4 0.1 reduce.1
  43.5 0.7 sub.20
  44.2 0.1 convert_reduce_fusion.2
  44.3 0.8 select_reduce_fusion.1
  45.0 0.1 reshape.169
  45.2 0.1 squeeze.11
  45.3 0.1 copy.25
  45.4 0.1 copy.26
  45.5 5.4 %all-to-all-done.1 = bf16[8,72,128]{2,1,0:T(8,128)(2,1)S(1)} async-done(((bf16[8,72,128]{2,1,0:T(8,128)(2,1)}), bf16[8,72,128]{2,1,0:T(8,128)(2,1)S(1)}, u32[]{:S(2)}, u32[]{:S(2)}) %all-to-all-start.1) | async-done | bytes 147488 | tf_op jit(solution)/shard_map/all_to_all | solution.py:255
  50.9 0.6 gather_fusion
  51.5 0.8 broadcast_select_fusion
  52.3 3.4 %all-to-all-start.2 = ((bf16[8,2,72,128]{3,2,1,0:T(8,128)(2,1)}), bf16[8,2,72,128]{3,2,1,0:T(8,128)(2,1)S(1)}, u32[]{:S(2)}, u32[]{:S(2)}) async-start(bf16[8,2,72,128]{3,2,1,0:T(8,128)(2,1)} %broadcast_select_fusion), calls=%async_computation.2 | async-start | bytes 589824 | tf_op jit(solution)/shard_map/all_to_all | solution.py:255
  55.8 0.1 and_select_fusion.4
  55.9 9.6 %all-to-all-done.2 = bf16[8,2,72,128]{3,2,1,0:T(8,128)(2,1)S(1)} async-done(((bf16[8,2,72,128]{3,2,1,0:T(8,128)(2,1)}), bf16[8,2,72,128]{3,2,1,0:T(8,128)(2,1)S(1)}, u32[]{:S(2)}, u32[]{:S(2)}) %all-to-all-start.2) | async-done | bytes 294944 | tf_op jit(solution)/shard_map/all_to_all | solution.py:255
  65.5 0.1 select_reduce_fusion
  65.6 0.8 broadcast_in_dim.74
  66.4 9.5 %all-to-all-start.3 = ((bf16[8,2,72,128]{3,2,1,0:T(8,128)(2,1)}), bf16[8,2,72,128]{3,2,1,0:T(8,128)(2,1)S(1)}, u32[]{:S(2)}, u32[]{:S(2)}) async-start(bf16[8,2,72,128]{3,2,1,0:T(8,128)(2,1)} %broadcast_in_dim.74), calls=%async_computation.3 | async-start | bytes 589824 | tf_op jit(solution)/shard_map/all_to_all | solution.py:255
  75.9 0.1 dynamic_slice.16.rlen
  76.0 0.1 dynamic_slice.20.plen
  76.0 6.7 %all-to-all-done.3 = bf16[8,2,72,128]{3,2,1,0:T(8,128)(2,1)S(1)} async-done(((bf16[8,2,72,128]{3,2,1,0:T(8,128)(2,1)}), bf16[8,2,72,128]{3,2,1,0:T(8,128)(2,1)S(1)}, u32[]{:S(2)}, u32[]{:S(2)}) %all-to-all-start.3) | async-done | bytes 294944 | tf_op jit(solution)/shard_map/all_to_all | solution.py:255
  82.7 0.3 both_keys.1
  83.1 0.8 copy-done.1
  83.9 0.8 copy-done.3
  84.7 6.6 %all-gather.2.cloned.1.call-done.wv_ref.wk_ref = bf16[512,4096]{1,0:T(8,128)(2,1)} async-done(((bf16[64,4096]{1,0:T(8,128)(2,1)}), bf16[512,4096]{1,0:T(8,128)(2,1)}) %all-gather.2.cloned.1.call-update) | async-done | bytes 4194320 | tf_op jit(solution)/shard_map/all_gather | solution.py:290
  91.3 11.3 %scores.1 = (bf16[576,384]{1,0:T(8,128)(2,1)S(1)}, bf16[2,1024,256]{2,1,0:T(8,128)(2,1)S(1)}, bf16[2,1024,256]{2,1,0:T(8,128)(2,1)S(1)}) custom-call(s32[2]{0:T(128)S(1)} %dynamic_slice.20.plen, s32[2]{0:T(128)S(1)} %dynamic_slice.16.rlen, bf16[128,3072]{1,0:T(8,128)(2,1)} %q_ref.1, bf16[128,2048]{1,0:T(8,128)(2,1)} %ct_ref.1, ...), custom_call_target="tpu_custom_call" | custom-call | flops 2818572288 | bytes 8388608 | tf_op jit(solution)/shard_map/scores/pallas_call | solution.py:164
  102.6 13.3 %all_to_all.36 = bf16[8,72,384]{2,1,0:T(8,128)(2,1)S(1)} all-to-all(bf16[8,72,384]{2,1,0:T(8,128)(2,1)S(1)} %bitcast.32), channel_id=1, replica_groups=mesh['resp'=64,'head'=8] {'head'}, dimensions={0} | all-to-all | bytes 884736 | tf_op jit(solution)/shard_map/all_to_all | solution.py:255
  115.9 0.1 convert_reduce_fusion
  115.9 0.7 broadcast_in_dim.76
  116.7 5.9 %all-to-all-start.5 = ((bf16[8,72,256]{2,1,0:T(8,128)(2,1)}), bf16[8,72,256]{2,1,0:T(8,128)(2,1)S(1)}, u32[]{:S(2)}, u32[]{:S(2)}) async-start(bf16[8,72,256]{2,1,0:T(8,128)(2,1)} %broadcast_in_dim.76), calls=%async_computation.5 | async-start | bytes 589824 | tf_op jit(solution)/shard_map/all_to_all | solution.py:255
  122.6 0.1 squeeze.12
  122.7 10.7 %all-to-all-done.5.in_ref = bf16[8,72,256]{2,1,0:T(8,128)(2,1)S(1)} async-done(((bf16[8,72,256]{2,1,0:T(8,128)(2,1)}), bf16[8,72,256]{2,1,0:T(8,128)(2,1)S(1)}, u32[]{:S(2)}, u32[]{:S(2)}) %all-to-all-start.5) | async-done | bytes 294944 | tf_op jit(solution)/shard_map/all_to_all | solution.py:255
  133.4 1.4 by_slot.1
  134.8 4.2 %all-to-all-start.6 = ((bf16[8,72,128]{2,1,0:T(8,128)(2,1)}), bf16[8,72,128]{2,1,0:T(8,128)(2,1)S(1)}, u32[]{:S(2)}, u32[]{:S(2)}) async-start(bf16[8,72,128]{2,1,0:T(8,128)(2,1)} %by_slot.1), calls=%async_computation.6 | async-start | bytes 294912 | tf_op jit(solution)/shard_map/all_to_all | solution.py:255
  139.0 6.7 %values.1 = (bf16[128,2048]{1,0:T(8,128)(2,1)}, bf16[128,3072]{1,0:T(8,128)(2,1)}) custom-call(s32[2]{0:T(128)S(1)} %dynamic_slice.16.rlen, bf16[512,4096]{1,0:T(8,128)(2,1)} %all-gather.2.cloned.1.call-done.wv_ref.wk_ref, bf16[512,4096]{1,0:T(8,128)(2,1)} %all-gather.2.cloned.1.call-done.wv_ref.wk_ref, bf16[2,256,640]{2,1,0:T(8,128)(2,1)} %copy-done.1, ...), custom_call_target="tpu_custom_call" | custom-call | flops 1677721600 | bytes 8388608 | tf_op jit(solution)/shard_map/values/pallas_call | solution.py:190
  145.6 0.6 slice_bitcast_fusion
  146.3 0.8 all-to-all-done.6
  147.1 0.6 convert_reduce_fusion.1
  (16 shorter events, 0.1 us)
Async XLA Ops:
  7.2 27.9 %copy-start = (bf16[1,128,576]{1,2,0:T(8,128)(2,1)S(1)}, bf16[1,128,576]{1,2,0:T(8,128)(2,1)}, u32[]{:S(2)}) copy-start(bf16[1,128,576]{1,2,0:T(8,128)(2,1)} %param.12) | copy-start | bytes 442372
  7.2 68.7 %copy-start.4 = (s32[128]{0:T(128)S(1)}, s32[128]{0:T(128)}, u32[]{:S(2)}) copy-start(s32[128]{0:T(128)} %param.17) | copy-start | bytes 1540
  7.2 75.5 %copy-start.2 = (bf16[128,576]{0,1:T(8,128)(2,1)S(1)}, bf16[128,576]{0,1:T(8,128)(2,1)}, u32[]{:S(2)}) copy-start(bf16[128,576]{0,1:T(8,128)(2,1)} %param.11) | copy-start | bytes 442372
  7.2 84.1 %all-gather.2.cloned.1.call-start = ((), (), s32[]{:S(2)}) async-start(), calls=%async_computation.7 | async-start | bytes 4718592 | tf_op jit(solution)/shard_map/all_gather | solution.py:290
  35.8 15.1 %all-to-all-start.1 = ((bf16[8,72,128]{2,1,0:T(8,128)(2,1)}), bf16[8,72,128]{2,1,0:T(8,128)(2,1)S(1)}, u32[]{:S(2)}, u32[]{:S(2)}) async-start(bf16[8,72,128]{2,1,0:T(8,128)(2,1)} %broadcast_in_dim.71), calls=%async_computation.1 | async-start | bytes 294912 | tf_op jit(solution)/shard_map/all_to_all | solution.py:255
  52.3 13.1 %all-to-all-start.2 = ((bf16[8,2,72,128]{3,2,1,0:T(8,128)(2,1)}), bf16[8,2,72,128]{3,2,1,0:T(8,128)(2,1)S(1)}, u32[]{:S(2)}, u32[]{:S(2)}) async-start(bf16[8,2,72,128]{3,2,1,0:T(8,128)(2,1)} %broadcast_select_fusion), calls=%async_computation.2 | async-start | bytes 589824 | tf_op jit(solution)/shard_map/all_to_all | solution.py:255
  66.4 16.3 %all-to-all-start.3 = ((bf16[8,2,72,128]{3,2,1,0:T(8,128)(2,1)}), bf16[8,2,72,128]{3,2,1,0:T(8,128)(2,1)S(1)}, u32[]{:S(2)}, u32[]{:S(2)}) async-start(bf16[8,2,72,128]{3,2,1,0:T(8,128)(2,1)} %broadcast_in_dim.74), calls=%async_computation.3 | async-start | bytes 589824 | tf_op jit(solution)/shard_map/all_to_all | solution.py:255
  83.0 0.8 copy-start.1
  83.9 0.8 copy-start.3
  116.7 16.7 %all-to-all-start.5 = ((bf16[8,72,256]{2,1,0:T(8,128)(2,1)}), bf16[8,72,256]{2,1,0:T(8,128)(2,1)S(1)}, u32[]{:S(2)}, u32[]{:S(2)}) async-start(bf16[8,72,256]{2,1,0:T(8,128)(2,1)} %broadcast_in_dim.76), calls=%async_computation.5 | async-start | bytes 589824 | tf_op jit(solution)/shard_map/all_to_all | solution.py:255
  134.8 12.3 %all-to-all-start.6 = ((bf16[8,72,128]{2,1,0:T(8,128)(2,1)}), bf16[8,72,128]{2,1,0:T(8,128)(2,1)S(1)}, u32[]{:S(2)}, u32[]{:S(2)}) async-start(bf16[8,72,128]{2,1,0:T(8,128)(2,1)} %by_slot.1), calls=%async_computation.6 | async-start | bytes 294912 | tf_op jit(solution)/shard_map/all_to_all | solution.py:255
Sparse Core Ops, SparseCore 0:
  35.2 56.0 all-gather.1

commit v3 on v2

--- a/solution.py
+++ b/solution.py
@@ -9,7 +9,7 @@
 from jax.sharding import PartitionSpec as P
 
 F32, BF16 = jnp.float32, jnp.bfloat16
-STEP_HEADS = 4
+SCORE_HEADS, VALUE_HEADS = 16, 8
 NT, TN = ((1,), (1,)), ((0,), (0,))
 
 
@@ -62,7 +62,7 @@
 
 def scores_kernel(
     sizes, plen, rlen, q_ref, ct_ref, wv_ref, wk_ref, kt_ref,
-    gk_ref, w_ref, gs_ref, qf_s, gl_s, acc_s,
+    gk_ref, w_ref, gs_ref, qf_s, gl_s, acc_s, bias_s,
 ):
     parts, rows, heads, nope, rope, val, lat, prows = sizes
     full, width = lat + rope, nope + rope
@@ -74,6 +74,12 @@
         qf_s[...] = jnp.zeros_like(qf_s)
         gl_s[...] = jnp.zeros_like(gl_s)
         acc_s[...] = jnp.zeros_like(acc_s)
+        for r in range(parts):
+            place = lax.broadcasted_iota(jnp.int32, bias_s.shape[1:], 0) % rows
+            key = lax.broadcasted_iota(jnp.int32, bias_s.shape[1:], 1)
+            own = key - (prows + r * rows)
+            valid = (key < plen[r]) | ((own >= 0) & (own <= place))
+            bias_s[r] = jnp.where(valid, 0.0, -jnp.inf)
 
     wv, wk, q, ct = wv_ref[...], wk_ref[...], q_ref[...], ct_ref[...]
     live = live_rows(rlen, parts, rows)
@@ -89,28 +95,23 @@
             qf_s[r, there, :lat] = q_lat[here]
             qf_s[r, there, lat:full] = q_rope[here]
             gl_s[r, there, :lat] = g_lat[here]
-    block, keys = heads * rows, kt_ref.shape[2]
+    raw = [dot(qf_s[r], kt_ref[r]) for r in range(parts)]
+    heard = [dot(gl_s[r, :, :lat], kt_ref[r, :lat]) for r in range(parts)]
     for r in range(parts):
-        qf, gl = qf_s[r], gl_s[r]
-        scores = dot(qf, kt_ref[r]) * scale
-        place = lax.broadcasted_iota(jnp.int32, (block, keys), 0) % rows
-        key = lax.broadcasted_iota(jnp.int32, (block, keys), 1)
-        own = key - (prows + r * rows)
-        valid = (key < plen[r]) | ((own >= 0) & (own <= place))
-        scores = jnp.where(valid, scores, -jnp.inf)
+        scores = raw[r] * scale + bias_s[r]
         expo = jnp.exp(scores - jnp.max(scores, axis=1, keepdims=True))
-        weights = expo / jnp.sum(expo, axis=1, keepdims=True)
-        weights_bf = weights.astype(BF16)
-        grad_w = dot(gl[:, :lat], kt_ref[r, :lat])
-        inner = jnp.sum(weights * grad_w, axis=1, keepdims=True)
-        grad_s = (weights * (grad_w - inner) * scale).astype(BF16)
-        w_ref[r] = weights_bf
-        gs_ref[r] = grad_s
-        both = jnp.concatenate([grad_s, weights_bf], axis=0)
-        rest = jnp.concatenate([qf, gl], axis=0)
-        grad_k = dot(both, rest, TN)
-        acc_s[r * prows : (r + 1) * prows] += grad_k[:prows]
+        weights = expo * (1.0 / jnp.sum(expo, axis=1, keepdims=True))
+        inner = jnp.sum(weights * heard[r], axis=1, keepdims=True)
+        w_ref[r] = weights.astype(BF16)
+        gs_ref[r] = (weights * (heard[r] - inner) * scale).astype(BF16)
+    for r in range(parts):
+        grad_k = dot(gs_ref[r], qf_s[r], TN)
+        grad_v = dot(w_ref[r], gl_s[r, :, :lat], TN)
+        at = slice(r * prows, (r + 1) * prows)
+        acc_s[at] += grad_k[:prows]
         acc_s[parts * prows :] += grad_k[prows:]
+        acc_s[at, :lat] += grad_v[:prows]
+        acc_s[parts * prows :, :lat] += grad_v[prows:]
 
     @pl.when(step == pl.num_programs(0) - 1)
     def _():
@@ -145,15 +146,21 @@
     heads = queries.shape[1] // width
     val = cotangent.shape[1] // heads
     rows = tokens // parts
-    hs = STEP_HEADS
-    steps = heads // hs
+    hs, vs = SCORE_HEADS, VALUE_HEADS
     sizes = (parts, rows, hs, nope, rope, val, lat, prows)
-    wv_spec = pl.BlockSpec((lat, hs * val), lambda i, *_: (0, i))
-    wk_spec = pl.BlockSpec((lat, hs * nope), lambda i, *_: (0, i + steps))
-    q_spec = pl.BlockSpec((tokens, hs * width), lambda i, *_: (0, i))
-    v_spec = pl.BlockSpec((tokens, hs * val), lambda i, *_: (0, i))
-    w_spec = pl.BlockSpec((parts, hs * rows, keys), lambda i, *_: (0, i, 0))
     w_shape = jax.ShapeDtypeStruct((parts, heads * rows, keys), BF16)
+
+    def specs(count):
+        steps = heads // count
+        return (
+            pl.BlockSpec((lat, count * val), lambda i, *_: (0, i)),
+            pl.BlockSpec((lat, count * nope), lambda i, *_: (0, i + steps)),
+            pl.BlockSpec((tokens, count * width), lambda i, *_: (0, i)),
+            pl.BlockSpec((tokens, count * val), lambda i, *_: (0, i)),
+            pl.BlockSpec((parts, count * rows, keys), lambda i, *_: (0, i, 0)),
+        )
+
+    wv_spec, wk_spec, q_spec, v_spec, w_spec = specs(hs)
     params = pltpu.CompilerParams(
         dimension_semantics=("arbitrary",), vmem_limit_bytes=30 << 20
     )
@@ -170,13 +177,14 @@
         ),
         grid_spec=pltpu.PrefetchScalarGridSpec(
             num_scalar_prefetch=2,
-            grid=(steps,),
+            grid=(heads // hs,),
             in_specs=[q_spec, v_spec, wv_spec, wk_spec, whole(*kt.shape)],
             out_specs=[whole(full, parts * prows + tokens), w_spec, w_spec],
             scratch_shapes=[
                 pltpu.VMEM((parts, hs * rows, wide), BF16),
                 pltpu.VMEM((parts, hs * rows, wide), BF16),
                 pltpu.VMEM((parts * prows + tokens, wide), F32),
+                pltpu.VMEM((parts, hs * rows, keys), F32),
             ],
         ),
         compiler_params=params,
@@ -187,6 +195,8 @@
         ),
         name="scores",
     )(plen, rlen, queries, cotangent, weights, weights, kt)
+    wv_spec, wk_spec, q_spec, v_spec, w_spec = specs(vs)
+    sizes = (parts, rows, vs, nope, rope, val, lat, prows)
     attended, grad_query = pl.pallas_call(
         functools.partial(values_kernel, sizes),
         out_shape=(
@@ -195,7 +205,7 @@
         ),
         grid_spec=pltpu.PrefetchScalarGridSpec(
             num_scalar_prefetch=1,
-            grid=(steps,),
+            grid=(heads // vs,),
             in_specs=[wv_spec, wk_spec, whole(*k.shape), w_spec, w_spec],
             out_specs=[v_spec, q_spec],
         ),
@@ -331,6 +341,7 @@
     grad_prompt = summed[:, :split].astype(BF16)
     in_row = to_all(grad_prompt, side, "resp", along_z)
     place = jnp.where(row_slots % side == my_z, row_slots // side, side).reshape(-1)
+    place, attended = lax.optimization_barrier((place, attended))
     to_owner = by_slot(place, in_row, side, prompt_rows)
     at_owner = exchange(to_owner, "resp", along_y)
     at_owner = jnp.sum(at_owner.astype(F32), axis=0)

time: 157 us -> 154 us (0.981)
  Pallas kernels: 19.6 us -> 16.4 us
    pallas_call x1, Pallas kernels: 11.3 us -> 8.31 us  [attend(): pl.pallas_call(functools.partial(scores_kernel, sizes), out_shape=(jax.Sh...]
  transfers between devices with their start and end apart: 6 -> 6, of which waited for: 6 -> 6; matrix products, arithmetic and copies ran while one was open for 4% -> 4% of each run, Pallas kernels for 5% -> 4%
where the time goes in v3:
time: 154 us; the launch traced here: 152 us
  blocking collectives  40.2 us (26%)
  waiting for transfers between devices  40 us (26%)
  starting transfers between devices  29.9 us (19%)
  Pallas kernels  16.4 us (11%)
  between operations  14.2 us (9%)
  local copies, waits for them, and re-layouts  6.56 us (4%)
  other arithmetic  4.33 us (3%)
    all_to_all x2, blocking collectives, exchange(): lax.all_to_all(tiles, axis, 0, 0, axis_index_groups=groups, tiled=True)  40.2 us
    all_to_all x5, waiting for transfers between devices, exchange(): lax.all_to_all(tiles, axis, 0, 0, axis_index_groups=groups, tiled=True)  33.4 us
    all_to_all x5, starting transfers between devices, exchange(): lax.all_to_all(tiles, axis, 0, 0, axis_index_groups=groups, tiled=True)  29.8 us
    pallas_call x1, Pallas kernels, attend(): pl.pallas_call(functools.partial(scores_kernel, sizes), out_shape=(jax.Sh...  8.31 us
    all_gather x1, waiting for transfers between devices, body(): lax.all_gather(stripes, 'resp', axis=0, tiled=True, axis_index_groups=alo...  6.55 us
    pallas_call x1, Pallas kernels, attend(): pl.pallas_call(functools.partial(values_kernel, sizes), out_shape=(jax.Sh...  6.47 us
  transfers between devices with their start and end apart: 6, of which 6 were waited for; matrix products, arithmetic and copies ran while one was open for 4% of the time, Pallas kernels for 4%

profile of v3, /device:TPU:1, one launch (start us, length us, event | category | flops | bytes accessed | tf_op | source)
XLA Modules:
  0.0 151.6 jit_solution(6714010530294158963)
XLA Ops:
  7.2 0.0 copy-start
  7.2 0.0 copy-start.4
  7.2 0.0 all-gather.2.cloned.1.call-start
  7.2 0.9 pad_maximum_fusion
  8.1 0.1 broadcast_in_dim.68
  8.2 26.9 %all_to_all.35 = bf16[8,32,8,128]{3,2,1,0:T(8,128)(2,1)} all-to-all(bf16[8,32,8,128]{3,2,1,0:T(8,128)(2,1)S(1)} %broadcast_in_dim.68), channel_id=1, replica_groups={{0,8,16,24,32,40,48,56},{64,72,80,88,96,104,112,120},{128,136,144,152,1..., dimensions={0} | all-to-all | bytes 1048576 | tf_op jit(solution)/shard_map/all_to_all | solution.py:265
  35.1 0.0 all-gather.2.cloned.1.call-update
  35.1 0.7 broadcast_in_dim.71
  35.8 6.8 %all-to-all-start.1 = ((bf16[8,72,128]{2,1,0:T(8,128)(2,1)}), bf16[8,72,128]{2,1,0:T(8,128)(2,1)S(1)}, u32[]{:S(2)}, u32[]{:S(2)}) async-start(bf16[8,72,128]{2,1,0:T(8,128)(2,1)} %broadcast_in_dim.71), calls=%async_computation.1 | async-start | bytes 294912 | tf_op jit(solution)/shard_map/all_to_all | solution.py:265
  42.6 0.7 copy.24
  43.4 0.1 reduce-window.9
  43.4 0.1 reduce.1
  43.5 0.7 sub.20
  44.2 0.1 convert_reduce_fusion.2
  44.3 0.8 select_reduce_fusion.1
  45.0 0.1 reshape.168
  45.2 0.1 squeeze.12
  45.3 0.1 copy.25
  45.4 0.1 copy.26
  45.5 5.4 %all-to-all-done.1 = bf16[8,72,128]{2,1,0:T(8,128)(2,1)S(1)} async-done(((bf16[8,72,128]{2,1,0:T(8,128)(2,1)}), bf16[8,72,128]{2,1,0:T(8,128)(2,1)S(1)}, u32[]{:S(2)}, u32[]{:S(2)}) %all-to-all-start.1) | async-done | bytes 147488 | tf_op jit(solution)/shard_map/all_to_all | solution.py:265
  50.9 0.6 gather_fusion
  51.5 0.8 broadcast_select_fusion
  52.3 3.4 %all-to-all-start.2 = ((bf16[8,2,72,128]{3,2,1,0:T(8,128)(2,1)}), bf16[8,2,72,128]{3,2,1,0:T(8,128)(2,1)S(1)}, u32[]{:S(2)}, u32[]{:S(2)}) async-start(bf16[8,2,72,128]{3,2,1,0:T(8,128)(2,1)} %broadcast_select_fusion), calls=%async_computation.2 | async-start | bytes 589824 | tf_op jit(solution)/shard_map/all_to_all | solution.py:265
  55.8 0.1 and_select_fusion.2
  55.9 9.6 %all-to-all-done.2 = bf16[8,2,72,128]{3,2,1,0:T(8,128)(2,1)S(1)} async-done(((bf16[8,2,72,128]{3,2,1,0:T(8,128)(2,1)}), bf16[8,2,72,128]{3,2,1,0:T(8,128)(2,1)S(1)}, u32[]{:S(2)}, u32[]{:S(2)}) %all-to-all-start.2) | async-done | bytes 294944 | tf_op jit(solution)/shard_map/all_to_all | solution.py:265
  65.5 0.1 select_reduce_fusion
  65.6 0.8 broadcast_in_dim.74
  66.4 9.5 %all-to-all-start.3 = ((bf16[8,2,72,128]{3,2,1,0:T(8,128)(2,1)}), bf16[8,2,72,128]{3,2,1,0:T(8,128)(2,1)S(1)}, u32[]{:S(2)}, u32[]{:S(2)}) async-start(bf16[8,2,72,128]{3,2,1,0:T(8,128)(2,1)} %broadcast_in_dim.74), calls=%async_computation.3 | async-start | bytes 589824 | tf_op jit(solution)/shard_map/all_to_all | solution.py:265
  75.9 0.1 dynamic_slice.17.rlen
  76.0 0.1 dynamic_slice.20.plen
  76.0 6.7 %all-to-all-done.3 = bf16[8,2,72,128]{3,2,1,0:T(8,128)(2,1)S(1)} async-done(((bf16[8,2,72,128]{3,2,1,0:T(8,128)(2,1)}), bf16[8,2,72,128]{3,2,1,0:T(8,128)(2,1)S(1)}, u32[]{:S(2)}, u32[]{:S(2)}) %all-to-all-start.3) | async-done | bytes 294944 | tf_op jit(solution)/shard_map/all_to_all | solution.py:265
  82.7 0.3 both_keys.1
  83.1 0.8 copy-done.1
  83.9 0.8 copy-done.3
  84.7 6.6 %all-gather.2.cloned.1.call-done.wv_ref.wk_ref = bf16[512,4096]{1,0:T(8,128)(2,1)} async-done(((bf16[64,4096]{1,0:T(8,128)(2,1)}), bf16[512,4096]{1,0:T(8,128)(2,1)}) %all-gather.2.cloned.1.call-update) | async-done | bytes 4194320 | tf_op jit(solution)/shard_map/all_gather | solution.py:300
  91.3 8.3 %scores.1 = (bf16[576,384]{1,0:T(8,128)(2,1)S(1)}, bf16[2,1024,256]{2,1,0:T(8,128)(2,1)S(1)}, bf16[2,1024,256]{2,1,0:T(8,128)(2,1)S(1)}) custom-call(s32[2]{0:T(128)S(1)} %dynamic_slice.20.plen, s32[2]{0:T(128)S(1)} %dynamic_slice.17.rlen, bf16[128,3072]{1,0:T(8,128)(2,1)} %q_ref.1, bf16[128,2048]{1,0:T(8,128)(2,1)} %ct_ref.1, ...), custom_call_target="tpu_custom_call" | custom-call | flops 2818572288 | bytes 8388608 | tf_op jit(solution)/shard_map/scores/pallas_call | solution.py:171
  99.6 13.3 %all_to_all.36 = bf16[8,72,384]{2,1,0:T(8,128)(2,1)S(1)} all-to-all(bf16[8,72,384]{2,1,0:T(8,128)(2,1)S(1)} %bitcast.32), channel_id=1, replica_groups=mesh['resp'=64,'head'=8] {'head'}, dimensions={0} | all-to-all | bytes 884736 | tf_op jit(solution)/shard_map/all_to_all | solution.py:265
  112.9 0.1 convert_reduce_fusion
  113.0 0.7 broadcast_in_dim.76
  113.7 5.9 %all-to-all-start.5 = ((bf16[8,72,256]{2,1,0:T(8,128)(2,1)}), bf16[8,72,256]{2,1,0:T(8,128)(2,1)S(1)}, u32[]{:S(2)}, u32[]{:S(2)}) async-start(bf16[8,72,256]{2,1,0:T(8,128)(2,1)} %broadcast_in_dim.76), calls=%async_computation.5 | async-start | bytes 589824 | tf_op jit(solution)/shard_map/all_to_all | solution.py:265
  119.6 0.1 squeeze.10
  119.7 6.5 %values.1 = (bf16[128,2048]{1,0:T(8,128)(2,1)}, bf16[128,3072]{1,0:T(8,128)(2,1)}) custom-call(s32[2]{0:T(128)S(1)} %dynamic_slice.17.rlen, bf16[512,4096]{1,0:T(8,128)(2,1)} %all-gather.2.cloned.1.call-done.wv_ref.wk_ref, bf16[512,4096]{1,0:T(8,128)(2,1)} %all-gather.2.cloned.1.call-done.wv_ref.wk_ref, bf16[2,256,640]{2,1,0:T(8,128)(2,1)} %copy-done.1, ...), custom_call_target="tpu_custom_call" | custom-call | flops 1677721600 | bytes 8388608 | tf_op jit(solution)/shard_map/values/pallas_call | solution.py:200
  126.2 4.2 %all-to-all-done.5.in_ref = bf16[8,72,256]{2,1,0:T(8,128)(2,1)S(1)} async-done(((bf16[8,72,256]{2,1,0:T(8,128)(2,1)}), bf16[8,72,256]{2,1,0:T(8,128)(2,1)S(1)}, u32[]{:S(2)}, u32[]{:S(2)}) %all-to-all-start.5) | async-done | bytes 294944 | tf_op jit(solution)/shard_map/all_to_all | solution.py:265
  130.4 1.4 by_slot.1
  131.8 4.2 %all-to-all-start.6 = ((bf16[8,72,128]{2,1,0:T(8,128)(2,1)}), bf16[8,72,128]{2,1,0:T(8,128)(2,1)S(1)}, u32[]{:S(2)}, u32[]{:S(2)}) async-start(bf16[8,72,128]{2,1,0:T(8,128)(2,1)} %by_slot.1), calls=%async_computation.6 | async-start | bytes 294912 | tf_op jit(solution)/shard_map/all_to_all | solution.py:265
  136.0 0.6 slice_bitcast_fusion
  136.6 7.5 %all-to-all-done.6 = bf16[8,72,128]{2,1,0:T(8,128)(2,1)S(1)} async-done(((bf16[8,72,128]{2,1,0:T(8,128)(2,1)}), bf16[8,72,128]{2,1,0:T(8,128)(2,1)S(1)}, u32[]{:S(2)}, u32[]{:S(2)}) %all-to-all-start.6) | async-done | bytes 147488 | tf_op jit(solution)/shard_map/all_to_all | solution.py:265
  144.1 0.6 convert_reduce_fusion.1
  (16 shorter events, 0.1 us)
Async XLA Ops:
  7.2 27.9 %copy-start = (bf16[1,128,576]{1,2,0:T(8,128)(2,1)S(1)}, bf16[1,128,576]{1,2,0:T(8,128)(2,1)}, u32[]{:S(2)}) copy-start(bf16[1,128,576]{1,2,0:T(8,128)(2,1)} %param.12) | copy-start | bytes 442372
  7.2 68.7 %copy-start.4 = (s32[128]{0:T(128)S(1)}, s32[128]{0:T(128)}, u32[]{:S(2)}) copy-start(s32[128]{0:T(128)} %param.17) | copy-start | bytes 1540
  7.2 75.5 %copy-start.2 = (bf16[128,576]{0,1:T(8,128)(2,1)S(1)}, bf16[128,576]{0,1:T(8,128)(2,1)}, u32[]{:S(2)}) copy-start(bf16[128,576]{0,1:T(8,128)(2,1)} %param.11) | copy-start | bytes 442372
  7.2 84.1 %all-gather.2.cloned.1.call-start = ((), (), s32[]{:S(2)}) async-start(), calls=%async_computation.7 | async-start | bytes 4718592 | tf_op jit(solution)/shard_map/all_gather | solution.py:300
  35.8 15.1 %all-to-all-start.1 = ((bf16[8,72,128]{2,1,0:T(8,128)(2,1)}), bf16[8,72,128]{2,1,0:T(8,128)(2,1)S(1)}, u32[]{:S(2)}, u32[]{:S(2)}) async-start(bf16[8,72,128]{2,1,0:T(8,128)(2,1)} %broadcast_in_dim.71), calls=%async_computation.1 | async-start | bytes 294912 | tf_op jit(solution)/shard_map/all_to_all | solution.py:265
  52.3 13.1 %all-to-all-start.2 = ((bf16[8,2,72,128]{3,2,1,0:T(8,128)(2,1)}), bf16[8,2,72,128]{3,2,1,0:T(8,128)(2,1)S(1)}, u32[]{:S(2)}, u32[]{:S(2)}) async-start(bf16[8,2,72,128]{3,2,1,0:T(8,128)(2,1)} %broadcast_select_fusion), calls=%async_computation.2 | async-start | bytes 589824 | tf_op jit(solution)/shard_map/all_to_all | solution.py:265
  66.4 16.3 %all-to-all-start.3 = ((bf16[8,2,72,128]{3,2,1,0:T(8,128)(2,1)}), bf16[8,2,72,128]{3,2,1,0:T(8,128)(2,1)S(1)}, u32[]{:S(2)}, u32[]{:S(2)}) async-start(bf16[8,2,72,128]{3,2,1,0:T(8,128)(2,1)} %broadcast_in_dim.74), calls=%async_computation.3 | async-start | bytes 589824 | tf_op jit(solution)/shard_map/all_to_all | solution.py:265
  83.0 0.8 copy-start.1
  83.9 0.8 copy-start.3
  113.7 16.7 %all-to-all-start.5 = ((bf16[8,72,256]{2,1,0:T(8,128)(2,1)}), bf16[8,72,256]{2,1,0:T(8,128)(2,1)S(1)}, u32[]{:S(2)}, u32[]{:S(2)}) async-start(bf16[8,72,256]{2,1,0:T(8,128)(2,1)} %broadcast_in_dim.76), calls=%async_computation.5 | async-start | bytes 589824 | tf_op jit(solution)/shard_map/all_to_all | solution.py:265
  131.8 12.3 %all-to-all-start.6 = ((bf16[8,72,128]{2,1,0:T(8,128)(2,1)}), bf16[8,72,128]{2,1,0:T(8,128)(2,1)S(1)}, u32[]{:S(2)}, u32[]{:S(2)}) async-start(bf16[8,72,128]{2,1,0:T(8,128)(2,1)} %by_slot.1), calls=%async_computation.6 | async-start | bytes 294912 | tf_op jit(solution)/shard_map/all_to_all | solution.py:265
Sparse Core Ops, SparseCore 0:
  35.2 56.0 all-gather.1
